TPU v7x, 256 devices: a whole 4x4x8 slice. The times are simulated.
256 devices in a mesh: ens: 2 (over y_hi), time: 32 (over z, x), chan: 4 (over y_lo, core).
Axes of the slice: x: 4, y: 4 (y_hi: 2, y_lo: 2; y = y_hi * 2 + y_lo), z: 8, core: 2. Of those that a mesh axis runs over, the one named last changes fastest.
Arguments:
- decay_rate: float32 [4, 32768, 1024], P('ens', 'time', 'chan'), parts along dimension 0, may hold values from 0.2 to 2
- drive_in: bfloat16 [4, 32768, 1024], P('ens', 'time', 'chan'), parts along dimension 0, may hold values from -6 to 6
- gate_in: bfloat16 [4, 32768, 1024], P('ens', 'time', 'chan'), parts along dimension 0, may hold values from -6 to 6
- norm_gain: float32 [2048], P(('ens', 'chan')), parts along dimension 0, may hold values from 0.25 to 1.75
Outputs:
- mixed_out: bfloat16 [4, 32768, 1024], P('ens', 'time', 'chan'), parts along dimension 0
There are 2 independent parts, one for each index of `ens`. A program takes and returns all parts, laid end to end along the dimension named above; each array names one. Nothing has to cross between parts.
All inputs are finite; a program needn't handle non-finite values.
Results may differ from a plain program's by a relative error of at most 0.001.
Values sent between devices are 32-bit elements.
No kernel may reach another device: no remote copies, remote signals or barrier semaphores. Data moves between devices by JAX's collectives and lax.ppermute only.
A program may use at most 64 MiB of HBM per device.

v0:
```python
import jax
import jax.numpy as jnp
from jax import lax
from jax.sharding import Mesh
from jax.sharding import PartitionSpec as P

TIME = ("time_0", "time_1")


def neutral_like(value, identity):
    return jax.tree.map(
        lambda a, e: jnp.broadcast_to(jnp.asarray(e, a.dtype), a.shape), value, identity
    )


def carried_in(value, axes, combine, identity, reverse):
    before = start = neutral_like(value, identity)
    running = value
    for axis in reversed(axes):
        devices, position = lax.axis_size(axis), lax.axis_index(axis)
        pieces = jax.tree.map(lambda part: lax.all_gather(part, axis), running)
        inside, running = start, start
        for k in reversed(range(devices)) if reverse else range(devices):
            passed = k > position if reverse else k < position
            running = combine(running, jax.tree.map(lambda part: part[k], pieces))
            inside = jax.tree.map(lambda new, old: jnp.where(passed, new, old), running, inside)
        before = combine(inside, before)
    return before


def over_pieces(value, axis):
    parts = lax.all_gather(value, axis)
    return parts.sum(axis=0)


def join_pair(earlier, later):
    return (earlier[0] * later[0], later[0] * earlier[1] + later[1])


def on_device(decay_rate, drive_in, gate_in, norm_gain):
    total_length = decay_rate.shape[1] * lax.axis_size(TIME)
    keep = jnp.exp(-decay_rate / total_length)
    push = drive_in.astype(jnp.float32) * total_length ** (-0.5)
    steps = -decay_rate / total_length
    logs = jnp.sum(steps, axis=1, keepdims=True) - jnp.cumsum(steps, axis=1)
    later_logs = logs
    summary = (jnp.exp(jnp.sum(steps, axis=1)), jnp.sum(jnp.exp(later_logs) * push, axis=1))
    entering_forward = carried_in(
        summary, TIME, join_pair, (jnp.ones_like(keep[:, 0]), jnp.zeros_like(push[:, 0])), False
    )
    started = push.at[:, 0].add(keep[:, 0] * entering_forward[1])
    forward = lax.associative_scan(join_pair, (keep, started), axis=1)[1]
    steps = -decay_rate / total_length
    logs = jnp.cumsum(steps, axis=1)
    before_logs = logs - steps
    summary = (jnp.exp(logs[:, -1]), jnp.sum(jnp.exp(before_logs) * push, axis=1))
    entering_backward = carried_in(
        summary, TIME, join_pair, (jnp.ones_like(keep[:, 0]), jnp.zeros_like(push[:, 0])), True
    )
    started = push.at[:, -1].add(keep[:, -1] * entering_backward[1])
    backward = lax.associative_scan(join_pair, (keep, started), axis=1, reverse=True)[1]
    states = forward + backward
    gated = states * jax.nn.silu(gate_in.astype(jnp.float32))
    power = over_pieces(jnp.sum(gated * gated, axis=-1, keepdims=True), "chan") / (
        gated.shape[-1] * lax.axis_size("chan")
    )
    mixed_out = (gated * lax.rsqrt(power + 1e-06) * norm_gain).astype(jnp.bfloat16)
    return mixed_out


def solution(mesh):
    finer = Mesh(
        mesh.devices.reshape(mesh.shape["ens"], 8, 4, mesh.shape["chan"]),
        ("ens", "time_0", "time_1", "chan"),
    )
    in_specs = (
        P("ens", TIME, "chan"),
        P("ens", TIME, "chan"),
        P("ens", TIME, "chan"),
        P(("ens", "chan")),
    )
    out_specs = P("ens", TIME, "chan")
    return jax.shard_map(
        on_device, mesh=finer, in_specs=in_specs, out_specs=out_specs, check_vma=False
    )
```

profile of v0, /device:TPU:1, one launch (start us, length us, event | category | flops | bytes accessed | tf_op | source)
XLA Modules:
  0.0 363.0 jit_solution(3151391685839674871)
XLA Ops:
  0.0 1.9 fusion.41
  3.2 10.1 %all-gather.5 = f32[4,2,256]{2,1,0:T(2,128)S(1)} all-gather(f32[1,2,256]{2,1,0:T(2,128)S(1)} %exponential_bitcast_fusion), channel_id=2, replica_groups=mesh['ens'=2,'time_0'=8,'time_1'=4,'chan'=4] {'time_1'}, dimensions={0}, use_global_device_ids=true | all-gather | bytes 10240 | tf_op jit(solution)/shard_map/all_gather | solution.py:21
  13.4 1.7 broadcast_add_fusion
  17.1 8.9 %all-gather.2 = f32[8,1,256]{2,1,0:T(1,128)S(1)} all-gather(f32[2,1,256]{2,1,0:T(1,128)S(1)} %slice_exponential_fusion), channel_id=4, replica_groups=mesh['ens'=2,'time_0'=8,'time_1'=4,'chan'=4] {'time_1'}, dimensions={0}, use_global_device_ids=true | all-gather | bytes 10240 | tf_op jit(solution)/shard_map/all_gather | solution.py:21
  27.2 3.6 slice.705
  30.8 8.9 %slice.813 = f32[2,512,256]{2,1,0:T(8,128)} reverse(f32[2,512,256]{2,1,0:T(8,128)} %slice.705), dimensions={1} | reverse | bytes 2097152 | tf_op jit(solution)/shard_map/slice | solution.py:61
  39.7 5.2 %slice.807 = f32[2,512,256]{2,1,0:T(8,128)} reverse(f32[2,512,256]{2,1,0:T(8,128)S(1)} %slice.709), dimensions={1} | reverse | bytes 2097152 | tf_op jit(solution)/shard_map/slice | solution.py:61
  44.8 3.6 slice.805
  48.4 9.1 %slice.806 = f32[2,511,256]{2,1,0:T(8,128)} reverse(f32[2,511,256]{2,1,0:T(8,128)} %slice.805), dimensions={1} | reverse | bytes 2093056 | tf_op jit(solution)/shard_map/slice | solution.py:61
  57.5 3.6 %slice.704 = f32[2,511,256]{2,1,0:T(8,128)} slice(f32[2,1024,256]{2,1,0:T(8,128)S(1)} %get-tuple-element.33), slice={[0:2:1], [2:1024:2], [0:256:1]} | slice | bytes 2093056 | tf_op jit(solution)/shard_map/slice | solution.py:52
  61.2 3.4 multiply_reduce_fusion.2
  64.6 8.9 %all-gather.7 = f32[4,2,256]{2,1,0:T(2,128)S(1)} all-gather(f32[1,2,256]{2,1,0:T(2,128)S(1)} %bitcast.179), channel_id=5, replica_groups=mesh['ens'=2,'time_0'=8,'time_1'=4,'chan'=4] {'time_1'}, dimensions={0}, use_global_device_ids=true | all-gather | bytes 10240 | tf_op jit(solution)/shard_map/all_gather | solution.py:21
  73.6 8.9 %all-gather.6 = f32[4,2,256]{2,1,0:T(2,128)S(1)} all-gather(f32[1,2,256]{2,1,0:T(2,128)S(1)} %bitcast.178), channel_id=3, replica_groups=mesh['ens'=2,'time_0'=8,'time_1'=4,'chan'=4] {'time_1'}, dimensions={0}, use_global_device_ids=true | all-gather | bytes 10240 | tf_op jit(solution)/shard_map/all_gather | solution.py:21
  82.6 21.8 %all_gather.43 = f32[8,2,256]{2,1,0:T(2,128)S(1)} all-gather(f32[1,2,256]{2,1,0:T(2,128)S(1)} %copy.27), channel_id=1, replica_groups=mesh['ens'=2,'time_0'=8,'time_1'=4,'chan'=4] {'time_0'}, dimensions={0}, use_global_device_ids=true | all-gather | bytes 18432 | tf_op jit(solution)/shard_map/all_gather | solution.py:21
  104.3 18.1 %all_gather.40 = f32[8,2,256]{2,1,0:T(2,128)S(1)} all-gather(f32[1,2,256]{2,1,0:T(2,128)S(1)} %copy.12), channel_id=1, replica_groups=mesh['ens'=2,'time_0'=8,'time_1'=4,'chan'=4] {'time_0'}, dimensions={0}, use_global_device_ids=true | all-gather | bytes 18432 | tf_op jit(solution)/shard_map/all_gather | solution.py:21
  123.2 18.1 %all_gather.48 = f32[8,2,256]{2,1,0:T(2,128)S(1)} all-gather(f32[1,2,256]{2,1,0:T(2,128)S(1)} %copy.49), channel_id=1, replica_groups=mesh['ens'=2,'time_0'=8,'time_1'=4,'chan'=4] {'time_0'}, dimensions={0}, use_global_device_ids=true | all-gather | bytes 18432 | tf_op jit(solution)/shard_map/all_gather | solution.py:21
  141.4 18.1 %all_gather.45 = f32[8,2,256]{2,1,0:T(2,128)S(1)} all-gather(f32[1,2,256]{2,1,0:T(2,128)S(1)} %copy.36), channel_id=1, replica_groups=mesh['ens'=2,'time_0'=8,'time_1'=4,'chan'=4] {'time_0'}, dimensions={0}, use_global_device_ids=true | all-gather | bytes 18432 | tf_op jit(solution)/shard_map/all_gather | solution.py:21
  163.2 6.5 %slice.777 = f32[2,511,256]{2,1,0:T(8,128)} slice(f32[2,1024,256]{2,1,0:T(8,128)} %scatter-add.6), slice={[0:2:1], [2:1024:2], [0:256:1]} | slice | bytes 2093056 | tf_op jit(solution)/shard_map/slice | solution.py:52
  169.7 6.4 %slice.707 = f32[2,512,256]{2,1,0:T(8,128)} slice(f32[2,1024,256]{2,1,0:T(8,128)} %scatter-add.6), slice={[0:2:1], [1:1024:2], [0:256:1]} | slice | bytes 2097152 | tf_op jit(solution)/shard_map/slice | solution.py:52
  176.1 6.4 %slice.706 = f32[2,512,256]{2,1,0:T(8,128)} slice(f32[2,1024,256]{2,1,0:T(8,128)} %scatter-add.6), slice={[0:2:1], [0:1023:2], [0:256:1]} | slice | bytes 2097152 | tf_op jit(solution)/shard_map/slice | solution.py:52
  182.5 3.2 fusion.43
  186.7 4.2 %slice.715 = f32[2,256,256]{2,1,0:T(8,128)} slice(f32[2,512,256]{2,1,0:T(8,128)} %get-tuple-element.36), slice={[0:2:1], [0:511:2], [0:256:1]} | slice | bytes 1048576 | tf_op jit(solution)/shard_map/slice | solution.py:52
  190.9 4.1 %slice.711 = f32[2,256,256]{2,1,0:T(8,128)} slice(f32[2,512,256]{2,1,0:T(8,128)} %get-tuple-element.36), slice={[0:2:1], [1:512:2], [0:256:1]} | slice | bytes 1048576 | tf_op jit(solution)/shard_map/slice | solution.py:52
  195.0 4.2 %slice.710 = f32[2,255,256]{2,1,0:T(8,128)} slice(f32[2,512,256]{2,1,0:T(8,128)} %get-tuple-element.36), slice={[0:2:1], [2:512:2], [0:256:1]} | slice | bytes 1044480 | tf_op jit(solution)/shard_map/slice | solution.py:52
  199.1 2.2 slice.775
  201.3 2.1 slice.713
  203.5 2.2 slice.712
  205.6 1.7 fusion.45
  222.8 3.0 pad.143
  225.8 2.2 fusion.7
  230.3 5.3 %pad.144 = f32[2,1024,256]{2,1,0:T(8,128)} pad(f32[2,512,256]{2,1,0:T(8,128)} %pad_maximum_fusion, f32[]{:T(128)} %constant.88.clone.1), padding=0_0_0x0_1_1x0_0_0 | pad | bytes 3145732 | tf_op jit(solution)/shard_map/pad | solution.py:52
  235.6 3.5 pad.145
  240.2 5.4 %slice.882 = f32[2,511,256]{2,1,0:T(8,128)} reverse(f32[2,511,256]{2,1,0:T(8,128)S(1)} %slice.881), dimensions={1} | reverse | bytes 2093056 | tf_op jit(solution)/shard_map/slice | solution.py:61
  246.8 3.6 slice.808
  250.4 8.9 %slice.809 = f32[2,512,256]{2,1,0:T(8,128)} reverse(f32[2,512,256]{2,1,0:T(8,128)} %slice.808), dimensions={1} | reverse | bytes 2097152 | tf_op jit(solution)/shard_map/slice | solution.py:61
  259.3 5.2 %slice.811 = f32[2,512,256]{2,1,0:T(8,128)} reverse(f32[2,512,256]{2,1,0:T(8,128)S(1)} %slice.810), dimensions={1} | reverse | bytes 2097152 | tf_op jit(solution)/shard_map/slice | solution.py:61
  264.4 2.4 fusion.44
  267.6 2.2 slice.815
  271.2 2.2 slice.817
  273.3 2.2 slice.816
  284.4 1.5 fusion.6
  287.1 2.3 pad.164
  289.5 3.5 pad.165
  293.0 3.2 add.621
  296.2 16.8 %rev.2 = f32[2,1024,256]{2,1,0:T(8,128)} reverse(f32[2,1024,256]{2,1,0:T(8,128)} %add.621), dimensions={1} | reverse | bytes 4194304 | tf_op jit(solution)/shard_map/rev | solution.py:61
  313.0 4.3 %multiply_reduce_fusion = (f32[2,1024]{1,0:T(2,128)S(1)}, f32[2,1024,256]{2,1,0:T(8,128)}) fusion(bf16[2,1024,256]{2,1,0:T(8,128)(2,1)S(1)} %copy-done.10, f32[2,1024,256]{2,1,0:T(8,128)} %rev.2, f32[2,1024,256]{2,1,0:T(8,128)S(1)} %copy-done.4, f32[2,1024,256]{2,1,0:T(8,128)} %pad.145), kind=kLoop, calls=%fused_computation.9 | loop fusion | flops 5240832 | bytes 9445376 | tf_op jit(solution)/shard_map/reduce_sum | solution.py:64
  317.3 42.7 %all-gather.8 = f32[4,2,1024]{2,1,0:T(2,128)S(1)} all-gather(f32[1,2,1024]{2,1,0:T(2,128)S(1)} %bitcast.177), channel_id=6, replica_groups=mesh['ens'=2,'time_0'=8,'time_1'=4,'chan'=4] {'chan'}, dimensions={0}, use_global_device_ids=true | all-gather | bytes 40960 | tf_op jit(solution)/shard_map/all_gather | solution.py:32
  360.1 2.9 multiply_convert_fusion
  (253 shorter events, 41.3 us)
Async XLA Ops:
  1.9 55.7 %copy-start = (f32[2,1024,256]{2,1,0:T(8,128)}, f32[2,1024,256]{2,1,0:T(8,128)S(1)}, u32[]{:S(2)}) copy-start(f32[2,1024,256]{2,1,0:T(8,128)S(1)} %get-tuple-element.33) | copy-start | bytes 6291460
  3.2 10.1 %copy-start.2 = (f32[2,256,8,128]{1,2,3,0:T(8,128)}, f32[2,256,8,128]{1,2,3,0:T(8,128)S(1)}, u32[]{:S(2)}) copy-start(f32[2,256,8,128]{1,2,3,0:T(8,128)S(1)} %fusion.4) | copy-start | bytes 6291460
  15.8 1.3 copy-start.3
  185.7 1.0 copy-start.5
  186.7 12.5 %copy-start.6 = (f32[2,512,256]{2,1,0:T(8,128)S(1)}, f32[2,512,256]{2,1,0:T(8,128)}, u32[]{:S(2)}) copy-start(f32[2,512,256]{2,1,0:T(8,128)} %copy-done.5) | copy-start | bytes 3145732
  216.1 1.1 copy-start.11
  225.8 2.2 copy-start.1
  230.3 5.3 %copy-start.8 = (f32[2,512,256]{2,1,0:T(8,128)S(1)}, f32[2,512,256]{2,1,0:T(8,128)}, u32[]{:S(2)}) copy-start(f32[2,512,256]{2,1,0:T(8,128)} %add.571) | copy-start | bytes 3145732
  270.5 5.0 %copy-start.9 = (f32[2,256,256]{2,1,0:T(8,128)S(1)}, f32[2,256,256]{2,1,0:T(8,128)}, u32[]{:S(2)}) copy-start(f32[2,256,256]{2,1,0:T(8,128)} %slice.815) | copy-start | bytes 1572868
  283.0 1.5 copy-start.7
  296.2 16.8 %copy-start.4 = (f32[2,1024,256]{2,1,0:T(8,128)S(1)}, f32[2,1024,256]{2,1,0:T(8,128)}, u32[]{:S(2)}) copy-start(f32[2,1024,256]{2,1,0:T(8,128)} %pad.144) | copy-start | bytes 6291460
  296.2 16.8 %copy-start.10 = (bf16[2,1024,256]{2,1,0:T(8,128)(2,1)S(1)}, bf16[2,1024,256]{2,1,0:T(8,128)(2,1)}, u32[]{:S(2)}) copy-start(bf16[2,1024,256]{2,1,0:T(8,128)(2,1)} %param.10) | copy-start | bytes 3145732
  313.0 47.1 %copy-start.12 = (f32[256]{0:T(256)S(1)}, f32[256]{0:T(256)}, u32[]{:S(2)}) copy-start(f32[256]{0:T(256)} %param.11) | copy-start | bytes 3076
where the time goes:
time: 367 us; the launch traced here: 363 us
  local copies, waits for them, and re-layouts  161 us (44%)
  blocking collectives  156 us (43%)
  other arithmetic  45.1 us (12%)
    all_gather x8, blocking collectives, carried_in(): pieces = jax.tree.map(lambda part: lax.all_gather(part, axis), running)  113 us
    slice x63, local copies, waits for them, and re-layouts, on_device(): lax.associative_scan(join_pair, (keep, started), axis=1, reverse=True)[1]  63.3 us
    slice x59, local copies, waits for them, and re-layouts, on_device(): forward = lax.associative_scan(join_pair, (keep, started), axis=1)[1]  53.6 us
    all_gather x1, blocking collectives, over_pieces(): parts = lax.all_gather(value, axis)  42.7 us
    rev x1, local copies, waits for them, and re-layouts, on_device(): lax.associative_scan(join_pair, (keep, started), axis=1, reverse=True)[1]  16.8 us
    pad x18, local copies, waits for them, and re-layouts, on_device(): forward = lax.associative_scan(join_pair, (keep, started), axis=1)[1]  13.5 us
    mul x18, other arithmetic, join_pair(): return (earlier[0] * later[0], later[0] * earlier[1] + later[1])  12 us
    pad x18, local copies, waits for them, and re-layouts, on_device(): lax.associative_scan(join_pair, (keep, started), axis=1, reverse=True)[1]  7.84 us

commit v1 on v0

v1 whole, which is shorter than its diff:
```python
import functools

import jax
import jax.numpy as jnp
from jax import lax
from jax.experimental import pallas as pl
from jax.experimental.pallas import tpu as pltpu
from jax.sharding import PartitionSpec as P

BLOCK = 128


def triangle(strict):
    row = lax.broadcasted_iota(jnp.int32, (BLOCK, 2 * BLOCK), 0)
    col = lax.broadcasted_iota(jnp.int32, (BLOCK, 2 * BLOCK), 1)
    col = jnp.where(col >= BLOCK, col - BLOCK, col)
    keep = col < row if strict else col <= row
    return jnp.where(keep, 1.0, 0.0).astype(jnp.bfloat16)


def stacked(top, bottom):
    return jnp.concatenate([top, bottom], axis=0)


def local_kernel(total_length, decay, drive, gate, gl, ga, gb, send,
                 decay_v, drive_v, gate_v, tile, sems):
    batch, length, chans = decay.shape
    blocks = length // BLOCK
    me = lax.axis_index("time")
    pairs = ((decay, decay_v), (drive, drive_v), (gate, gate_v))

    def copy(which, step):
        b, i = step // blocks, step % blocks
        src, dst = pairs[which]
        rows = pl.ds(i * BLOCK, BLOCK)
        return pltpu.make_async_copy(
            src.at[b, rows, :], dst.at[b, rows, :], sems.at[which, step])

    order = [b * blocks + i for i in range(blocks) for b in range(batch)]
    for step in order:
        for which in range(3):
            copy(which, step).start()
    upto = triangle(False)
    before = triangle(True)
    dot = functools.partial(jnp.dot, preferred_element_type=jnp.float32)
    carry = [[jnp.zeros((1, chans), jnp.float32)] * 3 for _ in range(batch)]
    for step in order:
        b, i = step // blocks, step % blocks
        for which in range(3):
            copy(which, step).wait()
        rows = pl.ds(i * BLOCK, BLOCK)
        sum_c, sum_f, sum_b = carry[b]
        d = decay_v[b, rows, :] * (1.0 / total_length)
        high = d.astype(jnp.bfloat16)
        low = (d - high.astype(jnp.float32)).astype(jnp.bfloat16)
        c = dot(upto, stacked(high, low)) + sum_c
        cp = c - d
        x16 = drive_v[b, rows, :]
        x = x16.astype(jnp.float32)
        v = ((jnp.exp(c) - 1.0) * x).astype(jnp.bfloat16)
        w = ((jnp.exp(-cp) - 1.0) * x).astype(jnp.bfloat16)
        f = dot(upto, stacked(x16, v)) + sum_f
        q = dot(before, stacked(x16, w)) + sum_b
        a = jnp.exp(-c)
        e = jnp.exp(cp)
        g = gate_v[b, rows, :].astype(jnp.float32)
        g = g / (1.0 + jnp.exp(-g))
        gl[b, rows, :] = g * (a * f - e * q)
        ga[b, rows, :] = g * a
        gb[b, rows, :] = g * e
        last = slice(BLOCK - 1, BLOCK)
        carry[b] = [
            c[last], f[last],
            q[last] + x[last] + w[last].astype(jnp.float32)]
    half = chans // 2
    for b in range(batch):
        sum_c, sum_f, sum_b = carry[b]
        p = jnp.exp(-sum_c)
        out_f = p * sum_f
        for k in range(2):
            cols = slice(k * half, (k + 1) * half)
            r = 2 * b + k
            for side, val in ((0, out_f), (1, sum_b)):
                tile[side, r:r + 1, :] = p[:, cols]
                tile[side, 4 + r:5 + r, :] = val[:, cols]
    rightward, leftward = tile[0], tile[1]
    for k in range(send.shape[0]):
        send[k] = jnp.where(k > me, rightward, leftward)


def states_kernel(recv, gl, ga, gb, gated, power):
    batch, length, chans = gl.shape
    devices = recv.shape[0]
    me = lax.axis_index("time")
    fwd = jnp.zeros(recv.shape[1:], jnp.float32)
    bwd = fwd
    for j in range(devices):
        got = recv[j]
        fwd = jnp.where(j < me, pltpu.roll(got, 4, 0) * fwd + got, fwd)
        j = devices - 1 - j
        got = recv[j]
        bwd = jnp.where(j >= me, pltpu.roll(got, 4, 0) * bwd + got, bwd)
    half = chans // 2
    for b in range(batch):
        for i in range(length // BLOCK):
            rows = pl.ds(i * BLOCK, BLOCK)
            total = None
            for k in range(2):
                cols = pl.ds(k * half, half)
                r = 4 + 2 * b + k
                s = (gl[b, rows, cols] + ga[b, rows, cols] * fwd[r:r + 1]
                     + gb[b, rows, cols] * bwd[r:r + 1])
                gated[b, rows, cols] = s
                total = s * s if k == 0 else total + s * s
            power[b, i:i + 1, :] = jnp.sum(total.T, axis=0, keepdims=True)


def scale_kernel(count, scale, gated, own, p1, p2, p3, gain, out):
    batch, length, chans = gated.shape
    half = chans // 2
    for b in range(batch):
        total = own[b] + p1[b] + p2[b] + p3[b]
        r = lax.rsqrt(total * (scale * scale / count) + 1e-06) * scale
        for i in range(length // BLOCK):
            rows = pl.ds(i * BLOCK, BLOCK)
            m = jnp.broadcast_to(r[i:i + 1, :], (BLOCK, BLOCK)).T
            for k in range(2):
                cols = pl.ds(k * half, half)
                out[b, rows, cols] = (
                    gated[b, rows, cols] * m * gain[:, cols]
                ).astype(jnp.bfloat16)


def on_device(decay_rate, drive_in, gate_in, norm_gain):
    batch, length, chans = decay_rate.shape
    devices = lax.axis_size("time")
    chan_devices = lax.axis_size("chan")
    total_length = length * devices
    steps = batch * (length // BLOCK)
    f32 = jnp.float32
    vmem = pl.BlockSpec(memory_space=pltpu.VMEM)
    hbm = pl.BlockSpec(memory_space=pltpu.HBM)
    full = jax.ShapeDtypeStruct((batch, length, chans), f32)
    gl, ga, gb, send = pl.pallas_call(
        functools.partial(local_kernel, total_length),
        out_shape=(full, full, full, jax.ShapeDtypeStruct((devices, 8, 128), f32)),
        in_specs=[hbm] * 3,
        out_specs=(vmem,) * 4,
        scratch_shapes=[
            pltpu.VMEM((batch, length, chans), f32),
            pltpu.VMEM((batch, length, chans), jnp.bfloat16),
            pltpu.VMEM((batch, length, chans), jnp.bfloat16),
            pltpu.VMEM((2, 8, 128), f32),
            pltpu.SemaphoreType.DMA((3, steps)),
        ],
        compiler_params=pltpu.CompilerParams(vmem_limit_bytes=32 << 20),
        name="local",
    )(*(pltpu.with_memory_space_constraint(a, pltpu.HBM)
        for a in (decay_rate, drive_in, gate_in)))
    recv = lax.all_to_all(send, "time", 0, 0)
    gated, power = pl.pallas_call(
        states_kernel,
        out_shape=(full, jax.ShapeDtypeStruct((batch, length // BLOCK, BLOCK), f32)),
        in_specs=[vmem] * 4,
        out_specs=(vmem,) * 2,
        compiler_params=pltpu.CompilerParams(vmem_limit_bytes=32 << 20),
        name="states",
    )(recv, gl, ga, gb)
    others = [
        lax.ppermute(power, "chan", [(i, i ^ k) for i in range(chan_devices)])
        for k in range(1, chan_devices)
    ]
    return pl.pallas_call(
        functools.partial(scale_kernel, chans * chan_devices, float(total_length) ** -0.5),
        out_shape=jax.ShapeDtypeStruct((batch, length, chans), jnp.bfloat16),
        in_specs=[vmem] * 6,
        out_specs=vmem,
        compiler_params=pltpu.CompilerParams(vmem_limit_bytes=32 << 20),
        name="scale",
    )(gated, power, *others, norm_gain.reshape(1, chans))


def solution(mesh):
    spec = P("ens", "time", "chan")
    return jax.shard_map(
        on_device, mesh=mesh, in_specs=(spec, spec, spec, P(("ens", "chan"))),
        out_specs=spec, check_vma=False,
    )
```

time: 367 us -> 36.5 us (0.10); the launches traced: 363 us -> 36.4 us
  local copies, waits for them, and re-layouts: 161 us -> 0.01 us
  blocking collectives: 156 us -> 21.1 us
  other arithmetic: 45.1 us -> 0 us
  Pallas kernels: 0 us -> 9.65 us
  starting transfers between devices: 0 us -> 3.7 us
    all_gather x9 -> x0, blocking collectives: 156 us -> none  [the longest x8 113 us: carried_in(): pieces = jax.tree.map(lambda part: lax.all_gather(part, axis), running)]
    slice x129 -> x0, local copies, waits for them, and re-layouts: 117 us -> none  [the longest x63 63.3 us: on_device(): lax.associative_scan(join_pair, (keep, started), axis=1, reverse=True)[1]]
    pad x36 -> x0, local copies, waits for them, and re-layouts: 21.4 us -> none  [the longest x18 13.5 us: on_device(): forward = lax.associative_scan(join_pair, (keep, started), axis=1)[1]]
    all_to_all x0 -> x1, blocking collectives: none -> 21.1 us  [on_device(): recv = lax.all_to_all(send, 'time', 0, 0)]
    rev x1 -> x0, local copies, waits for them, and re-layouts: 16.8 us -> none  [on_device(): lax.associative_scan(join_pair, (keep, started), axis=1, reverse=True)[1]]
    add x39 -> x0, other arithmetic: 13.5 us -> none  [the longest x18 5.5 us: join_pair(): return (earlier[0] * later[0], later[0] * earlier[1] + later[1])]
    mul x18 -> x0, other arithmetic: 12 us -> none  [join_pair(): return (earlier[0] * later[0], later[0] * earlier[1] + later[1])]
    pallas_call x0 -> x3, Pallas kernels: none -> 9.65 us  [the longest x1 7.75 us: on_device(): pl.pallas_call(functools.partial(local_kernel, total_length), out_shape=(...]
  transfers between devices with their start and end apart: 0 -> 3, of which waited for: 0 -> 2; matrix products, arithmetic and copies ran while one was open for 0% -> 0% of each run, Pallas kernels for 0% -> 0%
where the time goes in v1:
time: 36.5 us; the launch traced here: 36.4 us
  blocking collectives  21.1 us (58%)
  Pallas kernels  9.65 us (26%)
  starting transfers between devices  3.7 us (10%)
  waiting for transfers between devices  2.01 us (6%)
    all_to_all x1, blocking collectives, on_device(): recv = lax.all_to_all(send, 'time', 0, 0)  21.1 us
    pallas_call x1, Pallas kernels, on_device(): pl.pallas_call(functools.partial(local_kernel, total_length), out_shape=(...  7.75 us
    ppermute x3, starting transfers between devices, on_device(): lax.ppermute(power, 'chan', [(i, i ^ k) for i in range(chan_devices)])  3.7 us
    ppermute x3, waiting for transfers between devices, on_device(): lax.ppermute(power, 'chan', [(i, i ^ k) for i in range(chan_devices)])  2.01 us
    pallas_call x1, Pallas kernels, on_device(): pl.pallas_call(functools.partial(scale_kernel, chans * chan_devices, floa...  1.33 us
  transfers between devices with their start and end apart: 3, of which 2 were waited for; matrix products, arithmetic and copies ran while one was open for 0% of the time, Pallas kernels for 0%

profile of v1, /device:TPU:1, one launch (start us, length us, event | category | flops | bytes accessed | tf_op | source)
XLA Modules:
  0.0 36.4 jit_solution(8603581316122406299)
XLA Ops:
  0.0 7.7 %local.1 = (f32[2,1024,256]{2,1,0:T(8,128)S(1)}, f32[2,1024,256]{2,1,0:T(8,128)S(1)}, f32[2,1024,256]{2,1,0:T(8,128)S(1)}, f32[32,8,128]{2,1,0:T(8,128)S(1)}) custom-call(f32[2,1024,256]{2,1,0:T(8,128)} %decay.1, bf16[2,1024,256]{2,1,0:T(8,128)(2,1)} %drive.1, bf16[2,1024,256]{2,1,0:T(8,128)(2,1)} %gate.1), custom_call_target="tpu_custom_call" | custom-call | tf_op jit(solution)/shard_map/local/pallas_call | solution.py:144
  7.8 21.1 %all_to_all.5.recv = f32[32,8,128]{2,1,0:T(8,128)S(1)} all-to-all(f32[32,8,128]{2,1,0:T(8,128)S(1)} %get-tuple-element.11), channel_id=1, replica_groups=mesh['ens'=2,'time'=32,'chan'=4] {'time'}, dimensions={0} | all-to-all | bytes 262144 | tf_op jit(solution)/shard_map/all_to_all | solution.py:160
  28.8 0.0 copy-start
  28.8 0.6 %states.1 = (f32[2,1024,256]{2,1,0:T(8,128)S(1)}, f32[2,8,128]{2,1,0:T(8,128)S(1)}) custom-call(f32[32,8,128]{2,1,0:T(8,128)S(1)} %all_to_all.5.recv, f32[2,1024,256]{2,1,0:T(8,128)S(1)} %get-tuple-element.12.gl, f32[2,1024,256]{2,1,0:T(8,128)S(1)} %get-tuple-element.13.ga, f32[2,1024,256]{2,1,0:T(8,128)S(1)} %get-tuple-element.14.gb), custom_call_target="tpu_custom_call" | custom-call | tf_op jit(solution)/shard_map/states/pallas_call | solution.py:161
  29.4 3.2 %collective-permute-start.2 = (f32[2,8,128]{2,1,0:T(8,128)S(1)}, f32[2,8,128]{2,1,0:T(8,128)S(1)}, u32[]{:S(2)}, u32[]{:S(2)}) collective-permute-start(f32[2,8,128]{2,1,0:T(8,128)S(1)} %get-tuple-element.16.own), channel_id=1, source_target_pairs={{0,3},{1,2},{2,1},{3,0},{4,7},{5,6},{6,5},{7,4},{8,11},{9,10},{10,... | collective-permute-start | bytes 24584 | tf_op jit(solution)/shard_map/ppermute | solution.py:170
  32.6 0.2 collective-permute-start.1
  32.8 0.3 collective-permute-start
  33.1 1.0 %collective-permute-done.2.p3 = f32[2,8,128]{2,1,0:T(8,128)S(1)} collective-permute-done((f32[2,8,128]{2,1,0:T(8,128)S(1)}, f32[2,8,128]{2,1,0:T(8,128)S(1)}, u32[]{:S(2)}, u32[]{:S(2)}) %collective-permute-start.2) | collective-permute-done | bytes 8224 | tf_op jit(solution)/shard_map/ppermute | solution.py:170
  34.1 1.0 %collective-permute-done.1.p2 = f32[2,8,128]{2,1,0:T(8,128)S(1)} collective-permute-done((f32[2,8,128]{2,1,0:T(8,128)S(1)}, f32[2,8,128]{2,1,0:T(8,128)S(1)}, u32[]{:S(2)}, u32[]{:S(2)}) %collective-permute-start.1) | collective-permute-done | bytes 8224 | tf_op jit(solution)/shard_map/ppermute | solution.py:170
  35.1 0.0 collective-permute-done.p1
  35.1 0.0 copy-done
  35.1 1.3 %scale.1 = bf16[2,1024,256]{2,1,0:T(8,128)(2,1)} custom-call(f32[2,1024,256]{2,1,0:T(8,128)S(1)} %get-tuple-element.15.gated, f32[2,8,128]{2,1,0:T(8,128)S(1)} %get-tuple-element.16.own, f32[2,8,128]{2,1,0:T(8,128)S(1)} %collective-permute-done.p1, f32[2,8,128]{2,1,0:T(8,128)S(1)} %collective-permute-done.1.p2, f32[2,8,128]{2,1,0:T(8,128)S(1)} %collective-permute-done.2.p3, ...), custom_call_target="tpu_custom_call" | custom-call | tf_op jit(solution)/shard_map/scale/pallas_call | solution.py:173
Async XLA Ops:
  28.8 6.3 %copy-start = (f32[256]{0:T(256)S(1)}, f32[256]{0:T(256)}, u32[]{:S(2)}) copy-start(f32[256]{0:T(256)} %param.7) | copy-start | bytes 3076
  29.4 4.7 %collective-permute-start.2 = (f32[2,8,128]{2,1,0:T(8,128)S(1)}, f32[2,8,128]{2,1,0:T(8,128)S(1)}, u32[]{:S(2)}, u32[]{:S(2)}) collective-permute-start(f32[2,8,128]{2,1,0:T(8,128)S(1)} %get-tuple-element.16.own), channel_id=1, source_target_pairs={{0,3},{1,2},{2,1},{3,0},{4,7},{5,6},{6,5},{7,4},{8,11},{9,10},{10,... | collective-permute-start | bytes 24584 | tf_op jit(solution)/shard_map/ppermute | solution.py:170
  32.6 2.5 %collective-permute-start.1 = (f32[2,8,128]{2,1,0:T(8,128)S(1)}, f32[2,8,128]{2,1,0:T(8,128)S(1)}, u32[]{:S(2)}, u32[]{:S(2)}) collective-permute-start(f32[2,8,128]{2,1,0:T(8,128)S(1)} %get-tuple-element.16.own), channel_id=1, source_target_pairs={{0,2},{1,3},{2,0},{3,1},{4,6},{5,7},{6,4},{7,5},{8,10},{9,11},{10,... | collective-permute-start | bytes 24584 | tf_op jit(solution)/shard_map/ppermute | solution.py:170
  32.8 2.3 %collective-permute-start = (f32[2,8,128]{2,1,0:T(8,128)S(1)}, f32[2,8,128]{2,1,0:T(8,128)S(1)}, u32[]{:S(2)}, u32[]{:S(2)}) collective-permute-start(f32[2,8,128]{2,1,0:T(8,128)S(1)} %get-tuple-element.16.own), channel_id=1, source_target_pairs={{0,1},{1,0},{2,3},{3,2},{4,5},{5,4},{6,7},{7,6},{8,9},{9,8},{10,11... | collective-permute-start | bytes 24584 | tf_op jit(solution)/shard_map/ppermute | solution.py:170

commit v2 on v1

v2 whole, which is shorter than its diff:
```python
import functools

import jax
import jax.numpy as jnp
from jax import lax
from jax.experimental import pallas as pl
from jax.experimental.pallas import tpu as pltpu
from jax.sharding import PartitionSpec as P

BLOCK = 128
LOG2E = 1.4426950408889634


def triangle(strict):
    row = lax.broadcasted_iota(jnp.int32, (BLOCK, 2 * BLOCK), 0)
    col = lax.broadcasted_iota(jnp.int32, (BLOCK, 2 * BLOCK), 1)
    col = jnp.where(col >= BLOCK, col - BLOCK, col)
    keep = col < row if strict else col <= row
    return jnp.where(keep, 1.0, 0.0).astype(jnp.bfloat16)


def stacked(top, bottom):
    return jnp.concatenate([top, bottom], axis=0)


def local_kernel(total_length, decay, drive, a_out, e_out, f_out, q_out, ends, send,
                 decay_v, drive_v, c_v, v_v, w_v, tile, sems):
    batch, length, chans = decay.shape
    blocks = length // BLOCK
    me = lax.axis_index("time")
    unit = LOG2E / total_length
    pairs = ((decay, decay_v), (drive, drive_v))

    def copy(which, b, i):
        src, dst = pairs[which]
        rows = pl.ds(i * BLOCK, BLOCK)
        return pltpu.make_async_copy(
            src.at[b, rows, :], dst.at[b, rows, :], sems.at[which, b, i])

    for i in range(blocks):
        for b in range(batch):
            for which in range(2):
                copy(which, b, i).start()
    upto = triangle(False)
    before = triangle(True)
    dot = functools.partial(jnp.dot, preferred_element_type=jnp.float32)
    last = slice(BLOCK - 1, BLOCK)

    def prefix(b, i):
        rows = pl.ds(i * BLOCK, BLOCK)
        n = decay_v[b, rows, :] * -unit
        high = n.astype(jnp.bfloat16)
        low = (n - high.astype(jnp.float32)).astype(jnp.bfloat16)
        c_v[b, rows, :] = dot(upto, stacked(high, low))

    def weights(b, i):
        rows = pl.ds(i * BLOCK, BLOCK)
        d = decay_v[b, rows, :]
        c = c_v[b, rows, :]
        a = jnp.exp2(c)
        e = jnp.exp2(d * -unit - c)
        step = jnp.exp2(d * unit)
        a_out[b, rows, :] = a
        e_out[b, rows, :] = e
        x = drive_v[b, rows, :].astype(jnp.float32)
        v_v[b, rows, :] = ((e * step - 1.0) * x).astype(jnp.bfloat16)
        w_v[b, rows, :] = ((a * step - 1.0) * x).astype(jnp.bfloat16)
        ends[0, b, pl.ds(i, 1), :] = a[last]

    def sums(b, i):
        rows = pl.ds(i * BLOCK, BLOCK)
        x = drive_v[b, rows, :]
        w = w_v[b, rows, :]
        f = dot(upto, stacked(x, v_v[b, rows, :]))
        q = dot(before, stacked(x, w))
        f_out[b, rows, :] = f
        q_out[b, rows, :] = q
        ends[1, b, pl.ds(i, 1), :] = f[last]
        ends[2, b, pl.ds(i, 1), :] = (
            q[last] + x[last].astype(jnp.float32) + w[last].astype(jnp.float32))

    for s in range(blocks + 2):
        if s < blocks:
            for b in range(batch):
                for which in range(2):
                    copy(which, b, s).wait()
        for b in range(batch):
            if s >= 2:
                sums(b, s - 2)
            if 1 <= s <= blocks:
                weights(b, s - 1)
            if s < blocks:
                prefix(b, s)
    half = chans // 2
    for b in range(batch):
        fwd = bwd = jnp.zeros((1, chans), jnp.float32)
        p = jnp.ones((1, chans), jnp.float32)
        for i in range(blocks):
            j = blocks - 1 - i
            fwd = ends[0, b, i:i + 1, :] * (fwd + ends[1, b, i:i + 1, :])
            bwd = ends[2, b, j:j + 1, :] + ends[0, b, j:j + 1, :] * bwd
            p = p * ends[0, b, i:i + 1, :]
        for k in range(2):
            cols = slice(k * half, (k + 1) * half)
            r = 2 * b + k
            for side, val in ((0, fwd), (1, bwd)):
                tile[side, r:r + 1, :] = p[:, cols]
                tile[side, 4 + r:5 + r, :] = val[:, cols]
    rightward, leftward = tile[0], tile[1]
    for k in range(send.shape[0]):
        send[k] = jnp.where(k > me, rightward, leftward)


def states_kernel(recv, ends, a, e, f, q, gate, gated, power):
    batch, length, chans = a.shape
    blocks = length // BLOCK
    devices = recv.shape[0]
    me = lax.axis_index("time")
    fwd = jnp.zeros(recv.shape[1:], jnp.float32)
    bwd = fwd
    for j in range(devices):
        got = recv[j]
        fwd = jnp.where(j < me, pltpu.roll(got, 4, 0) * fwd + got, fwd)
        j = devices - 1 - j
        got = recv[j]
        bwd = jnp.where(j > me, pltpu.roll(got, 4, 0) * bwd + got, bwd)
    half = chans // 2
    for b in range(batch):
        alpha = [[None] * blocks for _ in range(2)]
        beta = [[None] * blocks for _ in range(2)]
        for k in range(2):
            cols = pl.ds(k * half, half)
            r = 4 + 2 * b + k
            state = fwd[r:r + 1]
            for i in range(blocks):
                alpha[k][i] = state
                state = ends[0, b, i:i + 1, cols] * (state + ends[1, b, i:i + 1, cols])
            state = bwd[r:r + 1]
            for i in reversed(range(blocks)):
                state = ends[2, b, i:i + 1, cols] + ends[0, b, i:i + 1, cols] * state
                beta[k][i] = state
        for i in range(blocks):
            rows = pl.ds(i * BLOCK, BLOCK)
            total = None
            for k in range(2):
                cols = pl.ds(k * half, half)
                h = gate[b, rows, cols].astype(jnp.float32) * 0.5
                s = (h + h * jnp.tanh(h)) * (
                    a[b, rows, cols] * (f[b, rows, cols] + alpha[k][i])
                    + e[b, rows, cols] * (beta[k][i] - q[b, rows, cols]))
                gated[b, rows, cols] = s
                total = s * s if k == 0 else total + s * s
            power[b, i:i + 1, :] = jnp.sum(total.T, axis=0, keepdims=True)


def scale_kernel(count, scale, gated, own, p1, p2, p3, gain, out, stage, sems):
    batch, length, chans = gated.shape
    half = chans // 2
    copies = []
    for b in range(batch):
        total = own[b] + p1[b] + p2[b] + p3[b]
        r = lax.rsqrt(total * (scale * scale / count) + 1e-06) * scale
        for i in range(length // BLOCK):
            rows = pl.ds(i * BLOCK, BLOCK)
            m = jnp.broadcast_to(r[i:i + 1, :], (BLOCK, BLOCK)).T
            for k in range(2):
                cols = pl.ds(k * half, half)
                stage[b, rows, cols] = (
                    gated[b, rows, cols] * m * gain[:, cols]
                ).astype(jnp.bfloat16)
            copies.append(pltpu.make_async_copy(
                stage.at[b, rows, :], out.at[b, rows, :], sems.at[b, i]))
            copies[-1].start()
    for c in copies:
        c.wait()


def on_device(decay_rate, drive_in, gate_in, norm_gain):
    batch, length, chans = decay_rate.shape
    blocks = length // BLOCK
    devices = lax.axis_size("time")
    chan_devices = lax.axis_size("chan")
    total_length = length * devices
    f32 = jnp.float32
    vmem = pl.BlockSpec(memory_space=pltpu.VMEM)
    hbm = pl.BlockSpec(memory_space=pltpu.HBM)
    full = jax.ShapeDtypeStruct((batch, length, chans), f32)
    a, e, f, q, ends, send = pl.pallas_call(
        functools.partial(local_kernel, total_length),
        out_shape=(full,) * 4 + (
            jax.ShapeDtypeStruct((3, batch, blocks, chans), f32),
            jax.ShapeDtypeStruct((devices, 8, 128), f32)),
        in_specs=[hbm] * 2,
        out_specs=(vmem,) * 6,
        scratch_shapes=[
            pltpu.VMEM((batch, length, chans), f32),
            pltpu.VMEM((batch, length, chans), jnp.bfloat16),
            pltpu.VMEM((batch, length, chans), f32),
            pltpu.VMEM((batch, length, chans), jnp.bfloat16),
            pltpu.VMEM((batch, length, chans), jnp.bfloat16),
            pltpu.VMEM((2, 8, 128), f32),
            pltpu.SemaphoreType.DMA((2, batch, blocks)),
        ],
        compiler_params=pltpu.CompilerParams(vmem_limit_bytes=32 << 20),
        name="local",
    )(*(pltpu.with_memory_space_constraint(t, pltpu.HBM)
        for t in (decay_rate, drive_in)))
    recv = lax.all_to_all(send, "time", 0, 0)
    gated, power = pl.pallas_call(
        states_kernel,
        out_shape=(full, jax.ShapeDtypeStruct((batch, blocks, BLOCK), f32)),
        in_specs=[vmem] * 7,
        out_specs=(vmem,) * 2,
        compiler_params=pltpu.CompilerParams(vmem_limit_bytes=32 << 20),
        name="states",
    )(recv, ends, a, e, f, q, gate_in)
    others = [
        lax.ppermute(power, "chan", [(i, i ^ k) for i in range(chan_devices)])
        for k in range(1, chan_devices)
    ]
    return pl.pallas_call(
        functools.partial(scale_kernel, chans * chan_devices, float(total_length) ** -0.5),
        out_shape=jax.ShapeDtypeStruct((batch, length, chans), jnp.bfloat16),
        in_specs=[vmem] * 6,
        out_specs=hbm,
        scratch_shapes=[
            pltpu.VMEM((batch, length, chans), jnp.bfloat16),
            pltpu.SemaphoreType.DMA((batch, blocks)),
        ],
        compiler_params=pltpu.CompilerParams(vmem_limit_bytes=32 << 20),
        name="scale",
    )(gated, power, *others, norm_gain.reshape(1, chans))


def solution(mesh):
    spec = P("ens", "time", "chan")
    return jax.shard_map(
        on_device, mesh=mesh, in_specs=(spec, spec, spec, P(("ens", "chan"))),
        out_specs=spec, check_vma=False,
    )
```

time: 36.5 us -> 34 us (0.932)
  Pallas kernels: 9.65 us -> 7.07 us
    pallas_call x1, Pallas kernels: 7.75 us -> 4.81 us  [on_device(): pl.pallas_call(functools.partial(local_kernel, total_length), out_shape=(...]
    pallas_call x1, Pallas kernels: 0.58 us -> 1.05 us  [on_device(): pl.pallas_call(states_kernel, out_shape=(full, jax.ShapeDtypeStruct((batc...]
where the time goes in v2:
time: 34 us; the launch traced here: 33.9 us
  blocking collectives  21.1 us (62%)
  Pallas kernels  7.07 us (21%)
  starting transfers between devices  3.71 us (11%)
  waiting for transfers between devices  2.01 us (6%)
    all_to_all x1, blocking collectives, on_device(): recv = lax.all_to_all(send, 'time', 0, 0)  21.1 us
    pallas_call x1, Pallas kernels, on_device(): pl.pallas_call(functools.partial(local_kernel, total_length), out_shape=(...  4.81 us
    ppermute x3, starting transfers between devices, on_device(): lax.ppermute(power, 'chan', [(i, i ^ k) for i in range(chan_devices)])  3.71 us
    ppermute x3, waiting for transfers between devices, on_device(): lax.ppermute(power, 'chan', [(i, i ^ k) for i in range(chan_devices)])  2.01 us
    pallas_call x1, Pallas kernels, on_device(): pl.pallas_call(functools.partial(scale_kernel, chans * chan_devices, floa...  1.21 us
    pallas_call x1, Pallas kernels, on_device(): pl.pallas_call(states_kernel, out_shape=(full, jax.ShapeDtypeStruct((batc...  1.05 us
  transfers between devices with their start and end apart: 3, of which 2 were waited for; matrix products, arithmetic and copies ran while one was open for 0% of the time, Pallas kernels for 0%

profile of v2, /device:TPU:1, one launch (start us, length us, event | category | flops | bytes accessed | tf_op | source)
XLA Modules:
  0.0 33.9 jit_solution(17465000611928034124)
XLA Ops:
  0.0 0.0 copy-start
  0.0 4.8 %local.1 = (f32[2,1024,256]{2,1,0:T(8,128)S(1)}, f32[2,1024,256]{2,1,0:T(8,128)S(1)}, f32[2,1024,256]{2,1,0:T(8,128)S(1)}, f32[2,1024,256]{2,1,0:T(8,128)S(1)}, ...) custom-call(f32[2,1024,256]{2,1,0:T(8,128)} %decay.1, bf16[2,1024,256]{2,1,0:T(8,128)(2,1)} %drive.1), custom_call_target="tpu_custom_call" | custom-call | tf_op jit(solution)/shard_map/local/pallas_call | solution.py:188
  4.8 21.1 %all_to_all.5.recv = f32[32,8,128]{2,1,0:T(8,128)S(1)} all-to-all(f32[32,8,128]{2,1,0:T(8,128)S(1)} %get-tuple-element.13), channel_id=1, replica_groups=mesh['ens'=2,'time'=32,'chan'=4] {'time'}, dimensions={0} | all-to-all | bytes 262144 | tf_op jit(solution)/shard_map/all_to_all | solution.py:208
  25.9 0.0 copy-done
  25.9 0.0 copy-start.1
  25.9 1.1 %states.1 = (f32[2,1024,256]{2,1,0:T(8,128)S(1)}, f32[2,8,128]{2,1,0:T(8,128)S(1)}) custom-call(f32[32,8,128]{2,1,0:T(8,128)S(1)} %all_to_all.5.recv, f32[3,2,8,256]{3,2,1,0:T(8,128)S(1)} %get-tuple-element.14.ends, f32[2,1024,256]{2,1,0:T(8,128)S(1)} %get-tuple-element.15.a, f32[2,1024,256]{2,1,0:T(8,128)S(1)} %get-tuple-element.16.e, ...), custom_call_target="tpu_custom_call" | custom-call | tf_op jit(solution)/shard_map/states/pallas_call | solution.py:209
  26.9 3.2 %collective-permute-start.2 = (f32[2,8,128]{2,1,0:T(8,128)S(1)}, f32[2,8,128]{2,1,0:T(8,128)S(1)}, u32[]{:S(2)}, u32[]{:S(2)}) collective-permute-start(f32[2,8,128]{2,1,0:T(8,128)S(1)} %get-tuple-element.20.own), channel_id=1, source_target_pairs={{0,3},{1,2},{2,1},{3,0},{4,7},{5,6},{6,5},{7,4},{8,11},{9,10},{10,... | collective-permute-start | bytes 24584 | tf_op jit(solution)/shard_map/ppermute | solution.py:218
  30.1 0.2 collective-permute-start.1
  30.3 0.3 collective-permute-start
  30.6 1.0 %collective-permute-done.2.p3 = f32[2,8,128]{2,1,0:T(8,128)S(1)} collective-permute-done((f32[2,8,128]{2,1,0:T(8,128)S(1)}, f32[2,8,128]{2,1,0:T(8,128)S(1)}, u32[]{:S(2)}, u32[]{:S(2)}) %collective-permute-start.2) | collective-permute-done | bytes 8224 | tf_op jit(solution)/shard_map/ppermute | solution.py:218
  31.6 1.0 %collective-permute-done.1.p2 = f32[2,8,128]{2,1,0:T(8,128)S(1)} collective-permute-done((f32[2,8,128]{2,1,0:T(8,128)S(1)}, f32[2,8,128]{2,1,0:T(8,128)S(1)}, u32[]{:S(2)}, u32[]{:S(2)}) %collective-permute-start.1) | collective-permute-done | bytes 8224 | tf_op jit(solution)/shard_map/ppermute | solution.py:218
  32.6 0.0 collective-permute-done.p1
  32.7 0.0 copy-done.1
  32.7 1.2 %scale.1 = bf16[2,1024,256]{2,1,0:T(8,128)(2,1)} custom-call(f32[2,1024,256]{2,1,0:T(8,128)S(1)} %get-tuple-element.19.gated, f32[2,8,128]{2,1,0:T(8,128)S(1)} %get-tuple-element.20.own, f32[2,8,128]{2,1,0:T(8,128)S(1)} %collective-permute-done.p1, f32[2,8,128]{2,1,0:T(8,128)S(1)} %collective-permute-done.1.p2, f32[2,8,128]{2,1,0:T(8,128)S(1)} %collective-permute-done.2.p3, ...), custom_call_target="tpu_custom_call" | custom-call | tf_op jit(solution)/shard_map/scale/pallas_call | solution.py:221
Async XLA Ops:
  0.0 25.9 %copy-start = (bf16[2,1024,256]{2,1,0:T(8,128)(2,1)S(1)}, bf16[2,1024,256]{2,1,0:T(8,128)(2,1)}, u32[]{:S(2)}) copy-start(bf16[2,1024,256]{2,1,0:T(8,128)(2,1)} %gate.1) | copy-start | bytes 3145732
  25.9 6.8 %copy-start.1 = (f32[256]{0:T(256)S(1)}, f32[256]{0:T(256)}, u32[]{:S(2)}) copy-start(f32[256]{0:T(256)} %param.7) | copy-start | bytes 3076
  26.9 4.7 %collective-permute-start.2 = (f32[2,8,128]{2,1,0:T(8,128)S(1)}, f32[2,8,128]{2,1,0:T(8,128)S(1)}, u32[]{:S(2)}, u32[]{:S(2)}) collective-permute-start(f32[2,8,128]{2,1,0:T(8,128)S(1)} %get-tuple-element.20.own), channel_id=1, source_target_pairs={{0,3},{1,2},{2,1},{3,0},{4,7},{5,6},{6,5},{7,4},{8,11},{9,10},{10,... | collective-permute-start | bytes 24584 | tf_op jit(solution)/shard_map/ppermute | solution.py:218
  30.1 2.5 %collective-permute-start.1 = (f32[2,8,128]{2,1,0:T(8,128)S(1)}, f32[2,8,128]{2,1,0:T(8,128)S(1)}, u32[]{:S(2)}, u32[]{:S(2)}) collective-permute-start(f32[2,8,128]{2,1,0:T(8,128)S(1)} %get-tuple-element.20.own), channel_id=1, source_target_pairs={{0,2},{1,3},{2,0},{3,1},{4,6},{5,7},{6,4},{7,5},{8,10},{9,11},{10,... | collective-permute-start | bytes 24584 | tf_op jit(solution)/shard_map/ppermute | solution.py:218
  30.3 2.3 %collective-permute-start = (f32[2,8,128]{2,1,0:T(8,128)S(1)}, f32[2,8,128]{2,1,0:T(8,128)S(1)}, u32[]{:S(2)}, u32[]{:S(2)}) collective-permute-start(f32[2,8,128]{2,1,0:T(8,128)S(1)} %get-tuple-element.20.own), channel_id=1, source_target_pairs={{0,1},{1,0},{2,3},{3,2},{4,5},{5,4},{6,7},{7,6},{8,9},{9,8},{10,11... | collective-permute-start | bytes 24584 | tf_op jit(solution)/shard_map/ppermute | solution.py:218

commit v3 on v2

--- a/solution.py
+++ b/solution.py
@@ -8,6 +8,8 @@
 from jax.sharding import PartitionSpec as P
 
 BLOCK = 128
+TILE = 16
+WAITS = (0, 1, 4)
 LOG2E = 1.4426950408889634
 
 
@@ -24,7 +26,7 @@
 
 
 def local_kernel(total_length, decay, drive, a_out, e_out, f_out, q_out, ends, send,
-                 decay_v, drive_v, c_v, v_v, w_v, tile, sems):
+                 decay_v, drive_v, n_v, c_v, v_v, w_v, tile, sems):
     batch, length, chans = decay.shape
     blocks = length // BLOCK
     me = lax.axis_index("time")
@@ -46,26 +48,31 @@
     dot = functools.partial(jnp.dot, preferred_element_type=jnp.float32)
     last = slice(BLOCK - 1, BLOCK)
 
+    def split(b, i):
+        for r in range(0, BLOCK, TILE):
+            n = decay_v[b, pl.ds(i * BLOCK + r, TILE), :] * -unit
+            high = n.astype(jnp.bfloat16)
+            low = (n - high.astype(jnp.float32)).astype(jnp.bfloat16)
+            n_v[b, i, pl.ds(r, TILE), :] = high
+            n_v[b, i, pl.ds(BLOCK + r, TILE), :] = low
+
     def prefix(b, i):
-        rows = pl.ds(i * BLOCK, BLOCK)
-        n = decay_v[b, rows, :] * -unit
-        high = n.astype(jnp.bfloat16)
-        low = (n - high.astype(jnp.float32)).astype(jnp.bfloat16)
-        c_v[b, rows, :] = dot(upto, stacked(high, low))
+        c_v[b, pl.ds(i * BLOCK, BLOCK), :] = dot(upto, n_v[b, i])
 
     def weights(b, i):
-        rows = pl.ds(i * BLOCK, BLOCK)
-        d = decay_v[b, rows, :]
-        c = c_v[b, rows, :]
-        a = jnp.exp2(c)
-        e = jnp.exp2(d * -unit - c)
-        step = jnp.exp2(d * unit)
-        a_out[b, rows, :] = a
-        e_out[b, rows, :] = e
-        x = drive_v[b, rows, :].astype(jnp.float32)
-        v_v[b, rows, :] = ((e * step - 1.0) * x).astype(jnp.bfloat16)
-        w_v[b, rows, :] = ((a * step - 1.0) * x).astype(jnp.bfloat16)
-        ends[0, b, pl.ds(i, 1), :] = a[last]
+        for r in range(0, BLOCK, TILE):
+            rows = pl.ds(i * BLOCK + r, TILE)
+            d = decay_v[b, rows, :]
+            c = c_v[b, rows, :]
+            a = jnp.exp2(c)
+            e = jnp.exp2(d * -unit - c)
+            step = jnp.exp2(d * unit)
+            a_out[b, rows, :] = a
+            e_out[b, rows, :] = e
+            x = drive_v[b, rows, :].astype(jnp.float32)
+            v_v[b, rows, :] = ((e * step - 1.0) * x).astype(jnp.bfloat16)
+            w_v[b, rows, :] = ((a * step - 1.0) * x).astype(jnp.bfloat16)
+        ends[0, b, pl.ds(i, 1), :] = a[TILE - 1:TILE]
 
     def sums(b, i):
         rows = pl.ds(i * BLOCK, BLOCK)
@@ -79,18 +86,23 @@
         ends[2, b, pl.ds(i, 1), :] = (
             q[last] + x[last].astype(jnp.float32) + w[last].astype(jnp.float32))
 
-    for s in range(blocks + 2):
-        if s < blocks:
-            for b in range(batch):
-                for which in range(2):
-                    copy(which, b, s).wait()
+    waits = {at: stop for at, stop in zip(WAITS, WAITS[1:] + (blocks,))}
+    for s in range(blocks + 3):
+        if s in waits:
+            for i in range(s, waits[s]):
+                for b in range(batch):
+                    for which in range(2):
+                        copy(which, b, i).wait()
         for b in range(batch):
-            if s >= 2:
-                sums(b, s - 2)
+            if s >= 3:
+                sums(b, s - 3)
             if 1 <= s <= blocks:
-                weights(b, s - 1)
+                prefix(b, s - 1)
+        for b in range(batch):
+            if 2 <= s <= blocks + 1:
+                weights(b, s - 2)
             if s < blocks:
-                prefix(b, s)
+                split(b, s)
     half = chans // 2
     for b in range(batch):
         fwd = bwd = jnp.zeros((1, chans), jnp.float32)
@@ -195,6 +207,7 @@
         scratch_shapes=[
             pltpu.VMEM((batch, length, chans), f32),
             pltpu.VMEM((batch, length, chans), jnp.bfloat16),
+            pltpu.VMEM((batch, blocks, 2 * BLOCK, chans), jnp.bfloat16),
             pltpu.VMEM((batch, length, chans), f32),
             pltpu.VMEM((batch, length, chans), jnp.bfloat16),
             pltpu.VMEM((batch, length, chans), jnp.bfloat16),

time: 34 us -> 33.1 us (0.974)
  Pallas kernels: 7.07 us -> 6.19 us
    pallas_call x1, Pallas kernels: 4.81 us -> 3.94 us  [on_device(): pl.pallas_call(functools.partial(local_kernel, total_length), out_shape=(...]
where the time goes in v3:
time: 33.1 us; the launch traced here: 33 us
  blocking collectives  21.1 us (64%)
  Pallas kernels  6.19 us (19%)
  starting transfers between devices  3.7 us (11%)
  waiting for transfers between devices  2.01 us (6%)
    all_to_all x1, blocking collectives, on_device(): recv = lax.all_to_all(send, 'time', 0, 0)  21.1 us
    pallas_call x1, Pallas kernels, on_device(): pl.pallas_call(functools.partial(local_kernel, total_length), out_shape=(...  3.94 us
    ppermute x3, starting transfers between devices, on_device(): lax.ppermute(power, 'chan', [(i, i ^ k) for i in range(chan_devices)])  3.7 us
    ppermute x3, waiting for transfers between devices, on_device(): lax.ppermute(power, 'chan', [(i, i ^ k) for i in range(chan_devices)])  2.01 us
    pallas_call x1, Pallas kernels, on_device(): pl.pallas_call(functools.partial(scale_kernel, chans * chan_devices, floa...  1.21 us
    pallas_call x1, Pallas kernels, on_device(): pl.pallas_call(states_kernel, out_shape=(full, jax.ShapeDtypeStruct((batc...  1.05 us
  transfers between devices with their start and end apart: 3, of which 2 were waited for; matrix products, arithmetic and copies ran while one was open for 0% of the time, Pallas kernels for 0%

profile of v3, /device:TPU:1, one launch (start us, length us, event | category | flops | bytes accessed | tf_op | source)
XLA Modules:
  0.0 33.0 jit_solution(903531686249944254)
XLA Ops:
  0.0 0.0 copy-start
  0.0 3.9 %local.1 = (f32[2,1024,256]{2,1,0:T(8,128)S(1)}, f32[2,1024,256]{2,1,0:T(8,128)S(1)}, f32[2,1024,256]{2,1,0:T(8,128)S(1)}, f32[2,1024,256]{2,1,0:T(8,128)S(1)}, ...) custom-call(f32[2,1024,256]{2,1,0:T(8,128)} %decay.1, bf16[2,1024,256]{2,1,0:T(8,128)(2,1)} %drive.1), custom_call_target="tpu_custom_call" | custom-call | tf_op jit(solution)/shard_map/local/pallas_call | solution.py:200
  3.9 21.1 %all_to_all.5.recv = f32[32,8,128]{2,1,0:T(8,128)S(1)} all-to-all(f32[32,8,128]{2,1,0:T(8,128)S(1)} %get-tuple-element.13), channel_id=1, replica_groups=mesh['ens'=2,'time'=32,'chan'=4] {'time'}, dimensions={0} | all-to-all | bytes 262144 | tf_op jit(solution)/shard_map/all_to_all | solution.py:221
  25.0 0.0 copy-done
  25.0 0.0 copy-start.1
  25.0 1.1 %states.1 = (f32[2,1024,256]{2,1,0:T(8,128)S(1)}, f32[2,8,128]{2,1,0:T(8,128)S(1)}) custom-call(f32[32,8,128]{2,1,0:T(8,128)S(1)} %all_to_all.5.recv, f32[3,2,8,256]{3,2,1,0:T(8,128)S(1)} %get-tuple-element.14.ends, f32[2,1024,256]{2,1,0:T(8,128)S(1)} %get-tuple-element.15.a, f32[2,1024,256]{2,1,0:T(8,128)S(1)} %get-tuple-element.16.e, ...), custom_call_target="tpu_custom_call" | custom-call | tf_op jit(solution)/shard_map/states/pallas_call | solution.py:222
  26.1 3.2 %collective-permute-start.2 = (f32[2,8,128]{2,1,0:T(8,128)S(1)}, f32[2,8,128]{2,1,0:T(8,128)S(1)}, u32[]{:S(2)}, u32[]{:S(2)}) collective-permute-start(f32[2,8,128]{2,1,0:T(8,128)S(1)} %get-tuple-element.20.own), channel_id=1, source_target_pairs={{0,3},{1,2},{2,1},{3,0},{4,7},{5,6},{6,5},{7,4},{8,11},{9,10},{10,... | collective-permute-start | bytes 24584 | tf_op jit(solution)/shard_map/ppermute | solution.py:231
  29.3 0.2 collective-permute-start.1
  29.4 0.3 collective-permute-start
  29.8 1.0 %collective-permute-done.2.p3 = f32[2,8,128]{2,1,0:T(8,128)S(1)} collective-permute-done((f32[2,8,128]{2,1,0:T(8,128)S(1)}, f32[2,8,128]{2,1,0:T(8,128)S(1)}, u32[]{:S(2)}, u32[]{:S(2)}) %collective-permute-start.2) | collective-permute-done | bytes 8224 | tf_op jit(solution)/shard_map/ppermute | solution.py:231
  30.8 1.0 %collective-permute-done.1.p2 = f32[2,8,128]{2,1,0:T(8,128)S(1)} collective-permute-done((f32[2,8,128]{2,1,0:T(8,128)S(1)}, f32[2,8,128]{2,1,0:T(8,128)S(1)}, u32[]{:S(2)}, u32[]{:S(2)}) %collective-permute-start.1) | collective-permute-done | bytes 8224 | tf_op jit(solution)/shard_map/ppermute | solution.py:231
  31.8 0.0 collective-permute-done.p1
  31.8 0.0 copy-done.1
  31.8 1.2 %scale.1 = bf16[2,1024,256]{2,1,0:T(8,128)(2,1)} custom-call(f32[2,1024,256]{2,1,0:T(8,128)S(1)} %get-tuple-element.19.gated, f32[2,8,128]{2,1,0:T(8,128)S(1)} %get-tuple-element.20.own, f32[2,8,128]{2,1,0:T(8,128)S(1)} %collective-permute-done.p1, f32[2,8,128]{2,1,0:T(8,128)S(1)} %collective-permute-done.1.p2, f32[2,8,128]{2,1,0:T(8,128)S(1)} %collective-permute-done.2.p3, ...), custom_call_target="tpu_custom_call" | custom-call | tf_op jit(solution)/shard_map/scale/pallas_call | solution.py:234
Async XLA Ops:
  0.0 25.0 %copy-start = (bf16[2,1024,256]{2,1,0:T(8,128)(2,1)S(1)}, bf16[2,1024,256]{2,1,0:T(8,128)(2,1)}, u32[]{:S(2)}) copy-start(bf16[2,1024,256]{2,1,0:T(8,128)(2,1)} %gate.1) | copy-start | bytes 3145732
  25.0 6.8 %copy-start.1 = (f32[256]{0:T(256)S(1)}, f32[256]{0:T(256)}, u32[]{:S(2)}) copy-start(f32[256]{0:T(256)} %param.7) | copy-start | bytes 3076
  26.1 4.7 %collective-permute-start.2 = (f32[2,8,128]{2,1,0:T(8,128)S(1)}, f32[2,8,128]{2,1,0:T(8,128)S(1)}, u32[]{:S(2)}, u32[]{:S(2)}) collective-permute-start(f32[2,8,128]{2,1,0:T(8,128)S(1)} %get-tuple-element.20.own), channel_id=1, source_target_pairs={{0,3},{1,2},{2,1},{3,0},{4,7},{5,6},{6,5},{7,4},{8,11},{9,10},{10,... | collective-permute-start | bytes 24584 | tf_op jit(solution)/shard_map/ppermute | solution.py:231
  29.3 2.5 %collective-permute-start.1 = (f32[2,8,128]{2,1,0:T(8,128)S(1)}, f32[2,8,128]{2,1,0:T(8,128)S(1)}, u32[]{:S(2)}, u32[]{:S(2)}) collective-permute-start(f32[2,8,128]{2,1,0:T(8,128)S(1)} %get-tuple-element.20.own), channel_id=1, source_target_pairs={{0,2},{1,3},{2,0},{3,1},{4,6},{5,7},{6,4},{7,5},{8,10},{9,11},{10,... | collective-permute-start | bytes 24584 | tf_op jit(solution)/shard_map/ppermute | solution.py:231
  29.4 2.3 %collective-permute-start = (f32[2,8,128]{2,1,0:T(8,128)S(1)}, f32[2,8,128]{2,1,0:T(8,128)S(1)}, u32[]{:S(2)}, u32[]{:S(2)}) collective-permute-start(f32[2,8,128]{2,1,0:T(8,128)S(1)} %get-tuple-element.20.own), channel_id=1, source_target_pairs={{0,1},{1,0},{2,3},{3,2},{4,5},{5,4},{6,7},{7,6},{8,9},{9,8},{10,11... | collective-permute-start | bytes 24584 | tf_op jit(solution)/shard_map/ppermute | solution.py:231

commit v4 on v3

--- a/solution.py
+++ b/solution.py
@@ -9,7 +9,7 @@
 
 BLOCK = 128
 TILE = 16
-WAITS = (0, 1, 4)
+WAITS = (0, 1, 3, 5)
 LOG2E = 1.4426950408889634
 
 
@@ -33,16 +33,17 @@
     unit = LOG2E / total_length
     pairs = ((decay, decay_v), (drive, drive_v))
 
-    def copy(which, b, i):
+    waits = {at: stop for at, stop in zip(WAITS, WAITS[1:] + (blocks,))}
+
+    def copy(which, i):
         src, dst = pairs[which]
-        rows = pl.ds(i * BLOCK, BLOCK)
+        rows = pl.ds(i * BLOCK, (waits[i] - i) * BLOCK)
         return pltpu.make_async_copy(
-            src.at[b, rows, :], dst.at[b, rows, :], sems.at[which, b, i])
-
-    for i in range(blocks):
-        for b in range(batch):
-            for which in range(2):
-                copy(which, b, i).start()
+            src.at[:, rows, :], dst.at[:, rows, :], sems.at[which, i])
+
+    for i in WAITS:
+        for which in range(2):
+            copy(which, i).start()
     upto = triangle(False)
     before = triangle(True)
     dot = functools.partial(jnp.dot, preferred_element_type=jnp.float32)
@@ -70,8 +71,9 @@
             a_out[b, rows, :] = a
             e_out[b, rows, :] = e
             x = drive_v[b, rows, :].astype(jnp.float32)
-            v_v[b, rows, :] = ((e * step - 1.0) * x).astype(jnp.bfloat16)
-            w_v[b, rows, :] = ((a * step - 1.0) * x).astype(jnp.bfloat16)
+            grown = x * step
+            v_v[b, rows, :] = (e * grown - x).astype(jnp.bfloat16)
+            w_v[b, rows, :] = (a * grown - x).astype(jnp.bfloat16)
         ends[0, b, pl.ds(i, 1), :] = a[TILE - 1:TILE]
 
     def sums(b, i):
@@ -86,13 +88,10 @@
         ends[2, b, pl.ds(i, 1), :] = (
             q[last] + x[last].astype(jnp.float32) + w[last].astype(jnp.float32))
 
-    waits = {at: stop for at, stop in zip(WAITS, WAITS[1:] + (blocks,))}
     for s in range(blocks + 3):
         if s in waits:
-            for i in range(s, waits[s]):
-                for b in range(batch):
-                    for which in range(2):
-                        copy(which, b, i).wait()
+            for which in range(2):
+                copy(which, s).wait()
         for b in range(batch):
             if s >= 3:
                 sums(b, s - 3)
@@ -132,10 +131,12 @@
     bwd = fwd
     for j in range(devices):
         got = recv[j]
-        fwd = jnp.where(j < me, pltpu.roll(got, 4, 0) * fwd + got, fwd)
+        fwd = (jnp.where(j < me, pltpu.roll(got, 4, 0), 1.0) * fwd
+               + jnp.where(j < me, got, 0.0))
         j = devices - 1 - j
         got = recv[j]
-        bwd = jnp.where(j > me, pltpu.roll(got, 4, 0) * bwd + got, bwd)
+        bwd = (jnp.where(j > me, pltpu.roll(got, 4, 0), 1.0) * bwd
+               + jnp.where(j > me, got, 0.0))
     half = chans // 2
     for b in range(batch):
         alpha = [[None] * blocks for _ in range(2)]
@@ -156,7 +157,7 @@
             total = None
             for k in range(2):
                 cols = pl.ds(k * half, half)
-                h = gate[b, rows, cols].astype(jnp.float32) * 0.5
+                h = (gate[b, rows, cols] * 0.5).astype(jnp.float32)
                 s = (h + h * jnp.tanh(h)) * (
                     a[b, rows, cols] * (f[b, rows, cols] + alpha[k][i])
                     + e[b, rows, cols] * (beta[k][i] - q[b, rows, cols]))
@@ -212,7 +213,7 @@
             pltpu.VMEM((batch, length, chans), jnp.bfloat16),
             pltpu.VMEM((batch, length, chans), jnp.bfloat16),
             pltpu.VMEM((2, 8, 128), f32),
-            pltpu.SemaphoreType.DMA((2, batch, blocks)),
+            pltpu.SemaphoreType.DMA((2, blocks)),
         ],
         compiler_params=pltpu.CompilerParams(vmem_limit_bytes=32 << 20),
         name="local",

time: 33.1 us -> 32.7 us (0.988)
  Pallas kernels: 6.19 us -> 5.82 us
    pallas_call x1, Pallas kernels: 3.94 us -> 3.57 us  [on_device(): pl.pallas_call(functools.partial(local_kernel, total_length), out_shape=(...]
where the time goes in v4:
time: 32.7 us; the launch traced here: 32.6 us
  blocking collectives  21.1 us (65%)
  Pallas kernels  5.82 us (18%)
  starting transfers between devices  3.71 us (11%)
  waiting for transfers between devices  2.01 us (6%)
    all_to_all x1, blocking collectives, on_device(): recv = lax.all_to_all(send, 'time', 0, 0)  21.1 us
    ppermute x3, starting transfers between devices, on_device(): lax.ppermute(power, 'chan', [(i, i ^ k) for i in range(chan_devices)])  3.71 us
    pallas_call x1, Pallas kernels, on_device(): pl.pallas_call(functools.partial(local_kernel, total_length), out_shape=(...  3.57 us
    ppermute x3, waiting for transfers between devices, on_device(): lax.ppermute(power, 'chan', [(i, i ^ k) for i in range(chan_devices)])  2.01 us
    pallas_call x1, Pallas kernels, on_device(): pl.pallas_call(functools.partial(scale_kernel, chans * chan_devices, floa...  1.21 us
    pallas_call x1, Pallas kernels, on_device(): pl.pallas_call(states_kernel, out_shape=(full, jax.ShapeDtypeStruct((batc...  1.05 us
  transfers between devices with their start and end apart: 3, of which 2 were waited for; matrix products, arithmetic and copies ran while one was open for 0% of the time, Pallas kernels for 0%

profile of v4, /device:TPU:1, one launch (start us, length us, event | category | flops | bytes accessed | tf_op | source)
XLA Modules:
  0.0 32.6 jit_solution(11779346103975349798)
XLA Ops:
  0.0 0.0 copy-start
  0.0 3.6 %local.1 = (f32[2,1024,256]{2,1,0:T(8,128)S(1)}, f32[2,1024,256]{2,1,0:T(8,128)S(1)}, f32[2,1024,256]{2,1,0:T(8,128)S(1)}, f32[2,1024,256]{2,1,0:T(8,128)S(1)}, ...) custom-call(f32[2,1024,256]{2,1,0:T(8,128)} %decay.1, bf16[2,1024,256]{2,1,0:T(8,128)(2,1)} %drive.1), custom_call_target="tpu_custom_call" | custom-call | tf_op jit(solution)/shard_map/local/pallas_call | solution.py:201
  3.6 21.1 %all_to_all.5.recv = f32[32,8,128]{2,1,0:T(8,128)S(1)} all-to-all(f32[32,8,128]{2,1,0:T(8,128)S(1)} %get-tuple-element.13), channel_id=1, replica_groups=mesh['ens'=2,'time'=32,'chan'=4] {'time'}, dimensions={0} | all-to-all | bytes 262144 | tf_op jit(solution)/shard_map/all_to_all | solution.py:222
  24.6 0.0 copy-done
  24.6 0.0 copy-start.1
  24.6 1.0 %states.1 = (f32[2,1024,256]{2,1,0:T(8,128)S(1)}, f32[2,8,128]{2,1,0:T(8,128)S(1)}) custom-call(f32[32,8,128]{2,1,0:T(8,128)S(1)} %all_to_all.5.recv, f32[3,2,8,256]{3,2,1,0:T(8,128)S(1)} %get-tuple-element.14.ends, f32[2,1024,256]{2,1,0:T(8,128)S(1)} %get-tuple-element.15.a, f32[2,1024,256]{2,1,0:T(8,128)S(1)} %get-tuple-element.16.e, ...), custom_call_target="tpu_custom_call" | custom-call | tf_op jit(solution)/shard_map/states/pallas_call | solution.py:223
  25.7 3.2 %collective-permute-start.2 = (f32[2,8,128]{2,1,0:T(8,128)S(1)}, f32[2,8,128]{2,1,0:T(8,128)S(1)}, u32[]{:S(2)}, u32[]{:S(2)}) collective-permute-start(f32[2,8,128]{2,1,0:T(8,128)S(1)} %get-tuple-element.20.own), channel_id=1, source_target_pairs={{0,3},{1,2},{2,1},{3,0},{4,7},{5,6},{6,5},{7,4},{8,11},{9,10},{10,... | collective-permute-start | bytes 24584 | tf_op jit(solution)/shard_map/ppermute | solution.py:232
  28.9 0.2 collective-permute-start.1
  29.1 0.3 %collective-permute-start = (f32[2,8,128]{2,1,0:T(8,128)S(1)}, f32[2,8,128]{2,1,0:T(8,128)S(1)}, u32[]{:S(2)}, u32[]{:S(2)}) collective-permute-start(f32[2,8,128]{2,1,0:T(8,128)S(1)} %get-tuple-element.20.own), channel_id=1, source_target_pairs={{0,1},{1,0},{2,3},{3,2},{4,5},{5,4},{6,7},{7,6},{8,9},{9,8},{10,11... | collective-permute-start | bytes 24584 | tf_op jit(solution)/shard_map/ppermute | solution.py:232
  29.4 1.0 %collective-permute-done.2.p3 = f32[2,8,128]{2,1,0:T(8,128)S(1)} collective-permute-done((f32[2,8,128]{2,1,0:T(8,128)S(1)}, f32[2,8,128]{2,1,0:T(8,128)S(1)}, u32[]{:S(2)}, u32[]{:S(2)}) %collective-permute-start.2) | collective-permute-done | bytes 8224 | tf_op jit(solution)/shard_map/ppermute | solution.py:232
  30.4 1.0 %collective-permute-done.1.p2 = f32[2,8,128]{2,1,0:T(8,128)S(1)} collective-permute-done((f32[2,8,128]{2,1,0:T(8,128)S(1)}, f32[2,8,128]{2,1,0:T(8,128)S(1)}, u32[]{:S(2)}, u32[]{:S(2)}) %collective-permute-start.1) | collective-permute-done | bytes 8224 | tf_op jit(solution)/shard_map/ppermute | solution.py:232
  31.4 0.0 collective-permute-done.p1
  31.4 0.0 copy-done.1
  31.4 1.2 %scale.1 = bf16[2,1024,256]{2,1,0:T(8,128)(2,1)} custom-call(f32[2,1024,256]{2,1,0:T(8,128)S(1)} %get-tuple-element.19.gated, f32[2,8,128]{2,1,0:T(8,128)S(1)} %get-tuple-element.20.own, f32[2,8,128]{2,1,0:T(8,128)S(1)} %collective-permute-done.p1, f32[2,8,128]{2,1,0:T(8,128)S(1)} %collective-permute-done.1.p2, f32[2,8,128]{2,1,0:T(8,128)S(1)} %collective-permute-done.2.p3, ...), custom_call_target="tpu_custom_call" | custom-call | tf_op jit(solution)/shard_map/scale/pallas_call | solution.py:235
Async XLA Ops:
  0.0 24.6 %copy-start = (bf16[2,1024,256]{2,1,0:T(8,128)(2,1)S(1)}, bf16[2,1024,256]{2,1,0:T(8,128)(2,1)}, u32[]{:S(2)}) copy-start(bf16[2,1024,256]{2,1,0:T(8,128)(2,1)} %gate.1) | copy-start | bytes 3145732
  24.6 6.8 %copy-start.1 = (f32[256]{0:T(256)S(1)}, f32[256]{0:T(256)}, u32[]{:S(2)}) copy-start(f32[256]{0:T(256)} %param.7) | copy-start | bytes 3076
  25.7 4.7 %collective-permute-start.2 = (f32[2,8,128]{2,1,0:T(8,128)S(1)}, f32[2,8,128]{2,1,0:T(8,128)S(1)}, u32[]{:S(2)}, u32[]{:S(2)}) collective-permute-start(f32[2,8,128]{2,1,0:T(8,128)S(1)} %get-tuple-element.20.own), channel_id=1, source_target_pairs={{0,3},{1,2},{2,1},{3,0},{4,7},{5,6},{6,5},{7,4},{8,11},{9,10},{10,... | collective-permute-start | bytes 24584 | tf_op jit(solution)/shard_map/ppermute | solution.py:232
  28.9 2.5 %collective-permute-start.1 = (f32[2,8,128]{2,1,0:T(8,128)S(1)}, f32[2,8,128]{2,1,0:T(8,128)S(1)}, u32[]{:S(2)}, u32[]{:S(2)}) collective-permute-start(f32[2,8,128]{2,1,0:T(8,128)S(1)} %get-tuple-element.20.own), channel_id=1, source_target_pairs={{0,2},{1,3},{2,0},{3,1},{4,6},{5,7},{6,4},{7,5},{8,10},{9,11},{10,... | collective-permute-start | bytes 24584 | tf_op jit(solution)/shard_map/ppermute | solution.py:232
  29.1 2.3 %collective-permute-start = (f32[2,8,128]{2,1,0:T(8,128)S(1)}, f32[2,8,128]{2,1,0:T(8,128)S(1)}, u32[]{:S(2)}, u32[]{:S(2)}) collective-permute-start(f32[2,8,128]{2,1,0:T(8,128)S(1)} %get-tuple-element.20.own), channel_id=1, source_target_pairs={{0,1},{1,0},{2,3},{3,2},{4,5},{5,4},{6,7},{7,6},{8,9},{9,8},{10,11... | collective-permute-start | bytes 24584 | tf_op jit(solution)/shard_map/ppermute | solution.py:232

commit v5 on v4

--- a/solution.py
+++ b/solution.py
@@ -10,6 +10,7 @@
 BLOCK = 128
 TILE = 16
 WAITS = (0, 1, 3, 5)
+OUT = (0, 1, 2, 3, 4, 5, 6, 7)
 LOG2E = 1.4426950408889634
 
 
@@ -52,13 +53,12 @@
     def split(b, i):
         for r in range(0, BLOCK, TILE):
             n = decay_v[b, pl.ds(i * BLOCK + r, TILE), :] * -unit
-            high = n.astype(jnp.bfloat16)
-            low = (n - high.astype(jnp.float32)).astype(jnp.bfloat16)
-            n_v[b, i, pl.ds(r, TILE), :] = high
-            n_v[b, i, pl.ds(BLOCK + r, TILE), :] = low
+            n_v[b, i, pl.ds(r, TILE), :] = n.astype(jnp.bfloat16)
+            part = n if r == 0 else part + n
+        ends[0, b, pl.ds(i, 1), :] = jnp.exp2(jnp.sum(part, axis=0, keepdims=True))
 
     def prefix(b, i):
-        c_v[b, pl.ds(i * BLOCK, BLOCK), :] = dot(upto, n_v[b, i])
+        c_v[b, pl.ds(i * BLOCK, BLOCK), :] = dot(upto[:, :BLOCK], n_v[b, i])
 
     def weights(b, i):
         for r in range(0, BLOCK, TILE):
@@ -74,7 +74,6 @@
             grown = x * step
             v_v[b, rows, :] = (e * grown - x).astype(jnp.bfloat16)
             w_v[b, rows, :] = (a * grown - x).astype(jnp.bfloat16)
-        ends[0, b, pl.ds(i, 1), :] = a[TILE - 1:TILE]
 
     def sums(b, i):
         rows = pl.ds(i * BLOCK, BLOCK)
@@ -157,7 +156,7 @@
             total = None
             for k in range(2):
                 cols = pl.ds(k * half, half)
-                h = (gate[b, rows, cols] * 0.5).astype(jnp.float32)
+                h = gate[b, rows, cols].astype(jnp.float32) * 0.5
                 s = (h + h * jnp.tanh(h)) * (
                     a[b, rows, cols] * (f[b, rows, cols] + alpha[k][i])
                     + e[b, rows, cols] * (beta[k][i] - q[b, rows, cols]))
@@ -168,22 +167,25 @@
 
 def scale_kernel(count, scale, gated, own, p1, p2, p3, gain, out, stage, sems):
     batch, length, chans = gated.shape
+    blocks = length // BLOCK
     half = chans // 2
+    total = own[...] + p1[...] + p2[...] + p3[...]
+    r = lax.rsqrt(total * (scale * scale / count) + 1e-06) * scale
     copies = []
-    for b in range(batch):
-        total = own[b] + p1[b] + p2[b] + p3[b]
-        r = lax.rsqrt(total * (scale * scale / count) + 1e-06) * scale
-        for i in range(length // BLOCK):
+    for start, stop in zip(OUT, OUT[1:] + (blocks,)):
+        for i in range(start, stop):
             rows = pl.ds(i * BLOCK, BLOCK)
-            m = jnp.broadcast_to(r[i:i + 1, :], (BLOCK, BLOCK)).T
-            for k in range(2):
-                cols = pl.ds(k * half, half)
-                stage[b, rows, cols] = (
-                    gated[b, rows, cols] * m * gain[:, cols]
-                ).astype(jnp.bfloat16)
-            copies.append(pltpu.make_async_copy(
-                stage.at[b, rows, :], out.at[b, rows, :], sems.at[b, i]))
-            copies[-1].start()
+            for b in range(batch):
+                m = jnp.broadcast_to(r[b, i:i + 1, :], (BLOCK, BLOCK)).T
+                for k in range(2):
+                    cols = pl.ds(k * half, half)
+                    stage[b, rows, cols] = (
+                        gated[b, rows, cols] * m * gain[:, cols]
+                    ).astype(jnp.bfloat16)
+        rows = pl.ds(start * BLOCK, (stop - start) * BLOCK)
+        copies.append(pltpu.make_async_copy(
+            stage.at[:, rows, :], out.at[:, rows, :], sems.at[len(copies)]))
+        copies[-1].start()
     for c in copies:
         c.wait()
 
@@ -208,7 +210,7 @@
         scratch_shapes=[
             pltpu.VMEM((batch, length, chans), f32),
             pltpu.VMEM((batch, length, chans), jnp.bfloat16),
-            pltpu.VMEM((batch, blocks, 2 * BLOCK, chans), jnp.bfloat16),
+            pltpu.VMEM((batch, blocks, BLOCK, chans), jnp.bfloat16),
             pltpu.VMEM((batch, length, chans), f32),
             pltpu.VMEM((batch, length, chans), jnp.bfloat16),
             pltpu.VMEM((batch, length, chans), jnp.bfloat16),
@@ -239,7 +241,7 @@
         out_specs=hbm,
         scratch_shapes=[
             pltpu.VMEM((batch, length, chans), jnp.bfloat16),
-            pltpu.SemaphoreType.DMA((batch, blocks)),
+            pltpu.SemaphoreType.DMA((blocks,)),
         ],
         compiler_params=pltpu.CompilerParams(vmem_limit_bytes=32 << 20),
         name="scale",

time: 32.7 us -> 32.5 us (level)
  no operation moved by 1% of the time
where the time goes in v5:
time: 32.5 us; the launch traced here: 32.4 us
  blocking collectives  21.1 us (65%)
  Pallas kernels  5.58 us (17%)
  starting transfers between devices  3.69 us (11%)
  waiting for transfers between devices  2.01 us (6%)
    all_to_all x1, blocking collectives, on_device(): recv = lax.all_to_all(send, 'time', 0, 0)  21.1 us
    ppermute x3, starting transfers between devices, on_device(): lax.ppermute(power, 'chan', [(i, i ^ k) for i in range(chan_devices)])  3.69 us
    pallas_call x1, Pallas kernels, on_device(): pl.pallas_call(functools.partial(local_kernel, total_length), out_shape=(...  3.39 us
    ppermute x3, waiting for transfers between devices, on_device(): lax.ppermute(power, 'chan', [(i, i ^ k) for i in range(chan_devices)])  2.01 us
    pallas_call x1, Pallas kernels, on_device(): pl.pallas_call(functools.partial(scale_kernel, chans * chan_devices, floa...  1.14 us
    pallas_call x1, Pallas kernels, on_device(): pl.pallas_call(states_kernel, out_shape=(full, jax.ShapeDtypeStruct((batc...  1.05 us
  transfers between devices with their start and end apart: 3, of which 2 were waited for; matrix products, arithmetic and copies ran while one was open for 0% of the time, Pallas kernels for 0%

profile of v5, /device:TPU:1, one launch (start us, length us, event | category | flops | bytes accessed | tf_op | source)
XLA Modules:
  0.0 32.4 jit_solution(16155890851857228404)
XLA Ops:
  0.0 0.0 copy-start
  0.0 3.4 %local.1 = (f32[2,1024,256]{2,1,0:T(8,128)S(1)}, f32[2,1024,256]{2,1,0:T(8,128)S(1)}, f32[2,1024,256]{2,1,0:T(8,128)S(1)}, f32[2,1024,256]{2,1,0:T(8,128)S(1)}, ...) custom-call(f32[2,1024,256]{2,1,0:T(8,128)} %decay.1, bf16[2,1024,256]{2,1,0:T(8,128)(2,1)} %drive.1), custom_call_target="tpu_custom_call" | custom-call | tf_op jit(solution)/shard_map/local/pallas_call | solution.py:203
  3.4 21.1 %all_to_all.5.recv = f32[32,8,128]{2,1,0:T(8,128)S(1)} all-to-all(f32[32,8,128]{2,1,0:T(8,128)S(1)} %get-tuple-element.13), channel_id=1, replica_groups=mesh['ens'=2,'time'=32,'chan'=4] {'time'}, dimensions={0} | all-to-all | bytes 262144 | tf_op jit(solution)/shard_map/all_to_all | solution.py:224
  24.5 0.0 copy-done
  24.5 0.0 copy-start.1
  24.5 1.0 %states.1 = (f32[2,1024,256]{2,1,0:T(8,128)S(1)}, f32[2,8,128]{2,1,0:T(8,128)S(1)}) custom-call(f32[32,8,128]{2,1,0:T(8,128)S(1)} %all_to_all.5.recv, f32[3,2,8,256]{3,2,1,0:T(8,128)S(1)} %get-tuple-element.14.ends, f32[2,1024,256]{2,1,0:T(8,128)S(1)} %get-tuple-element.15.a, f32[2,1024,256]{2,1,0:T(8,128)S(1)} %get-tuple-element.16.e, ...), custom_call_target="tpu_custom_call" | custom-call | tf_op jit(solution)/shard_map/states/pallas_call | solution.py:225
  25.5 3.2 %collective-permute-start.2 = (f32[2,8,128]{2,1,0:T(8,128)S(1)}, f32[2,8,128]{2,1,0:T(8,128)S(1)}, u32[]{:S(2)}, u32[]{:S(2)}) collective-permute-start(f32[2,8,128]{2,1,0:T(8,128)S(1)} %get-tuple-element.20.own), channel_id=1, source_target_pairs={{0,3},{1,2},{2,1},{3,0},{4,7},{5,6},{6,5},{7,4},{8,11},{9,10},{10,... | collective-permute-start | bytes 24584 | tf_op jit(solution)/shard_map/ppermute | solution.py:234
  28.7 0.2 collective-permute-start.1
  28.9 0.3 %collective-permute-start = (f32[2,8,128]{2,1,0:T(8,128)S(1)}, f32[2,8,128]{2,1,0:T(8,128)S(1)}, u32[]{:S(2)}, u32[]{:S(2)}) collective-permute-start(f32[2,8,128]{2,1,0:T(8,128)S(1)} %get-tuple-element.20.own), channel_id=1, source_target_pairs={{0,1},{1,0},{2,3},{3,2},{4,5},{5,4},{6,7},{7,6},{8,9},{9,8},{10,11... | collective-permute-start | bytes 24584 | tf_op jit(solution)/shard_map/ppermute | solution.py:234
  29.2 1.0 %collective-permute-done.2.p3 = f32[2,8,128]{2,1,0:T(8,128)S(1)} collective-permute-done((f32[2,8,128]{2,1,0:T(8,128)S(1)}, f32[2,8,128]{2,1,0:T(8,128)S(1)}, u32[]{:S(2)}, u32[]{:S(2)}) %collective-permute-start.2) | collective-permute-done | bytes 8224 | tf_op jit(solution)/shard_map/ppermute | solution.py:234
  30.2 1.0 %collective-permute-done.1.p2 = f32[2,8,128]{2,1,0:T(8,128)S(1)} collective-permute-done((f32[2,8,128]{2,1,0:T(8,128)S(1)}, f32[2,8,128]{2,1,0:T(8,128)S(1)}, u32[]{:S(2)}, u32[]{:S(2)}) %collective-permute-start.1) | collective-permute-done | bytes 8224 | tf_op jit(solution)/shard_map/ppermute | solution.py:234
  31.2 0.0 collective-permute-done.p1
  31.2 0.0 copy-done.1
  31.2 1.1 %scale.1 = bf16[2,1024,256]{2,1,0:T(8,128)(2,1)} custom-call(f32[2,1024,256]{2,1,0:T(8,128)S(1)} %get-tuple-element.19.gated, f32[2,8,128]{2,1,0:T(8,128)S(1)} %get-tuple-element.20.own, f32[2,8,128]{2,1,0:T(8,128)S(1)} %collective-permute-done.p1, f32[2,8,128]{2,1,0:T(8,128)S(1)} %collective-permute-done.1.p2, f32[2,8,128]{2,1,0:T(8,128)S(1)} %collective-permute-done.2.p3, ...), custom_call_target="tpu_custom_call" | custom-call | tf_op jit(solution)/shard_map/scale/pallas_call | solution.py:237
Async XLA Ops:
  0.0 24.5 %copy-start = (bf16[2,1024,256]{2,1,0:T(8,128)(2,1)S(1)}, bf16[2,1024,256]{2,1,0:T(8,128)(2,1)}, u32[]{:S(2)}) copy-start(bf16[2,1024,256]{2,1,0:T(8,128)(2,1)} %gate.1) | copy-start | bytes 3145732
  24.5 6.8 %copy-start.1 = (f32[256]{0:T(256)S(1)}, f32[256]{0:T(256)}, u32[]{:S(2)}) copy-start(f32[256]{0:T(256)} %param.7) | copy-start | bytes 3076
  25.5 4.7 %collective-permute-start.2 = (f32[2,8,128]{2,1,0:T(8,128)S(1)}, f32[2,8,128]{2,1,0:T(8,128)S(1)}, u32[]{:S(2)}, u32[]{:S(2)}) collective-permute-start(f32[2,8,128]{2,1,0:T(8,128)S(1)} %get-tuple-element.20.own), channel_id=1, source_target_pairs={{0,3},{1,2},{2,1},{3,0},{4,7},{5,6},{6,5},{7,4},{8,11},{9,10},{10,... | collective-permute-start | bytes 24584 | tf_op jit(solution)/shard_map/ppermute | solution.py:234
  28.7 2.5 %collective-permute-start.1 = (f32[2,8,128]{2,1,0:T(8,128)S(1)}, f32[2,8,128]{2,1,0:T(8,128)S(1)}, u32[]{:S(2)}, u32[]{:S(2)}) collective-permute-start(f32[2,8,128]{2,1,0:T(8,128)S(1)} %get-tuple-element.20.own), channel_id=1, source_target_pairs={{0,2},{1,3},{2,0},{3,1},{4,6},{5,7},{6,4},{7,5},{8,10},{9,11},{10,... | collective-permute-start | bytes 24584 | tf_op jit(solution)/shard_map/ppermute | solution.py:234
  28.9 2.3 %collective-permute-start = (f32[2,8,128]{2,1,0:T(8,128)S(1)}, f32[2,8,128]{2,1,0:T(8,128)S(1)}, u32[]{:S(2)}, u32[]{:S(2)}) collective-permute-start(f32[2,8,128]{2,1,0:T(8,128)S(1)} %get-tuple-element.20.own), channel_id=1, source_target_pairs={{0,1},{1,0},{2,3},{3,2},{4,5},{5,4},{6,7},{7,6},{8,9},{9,8},{10,11... | collective-permute-start | bytes 24584 | tf_op jit(solution)/shard_map/ppermute | solution.py:234

commit v6 on v5

--- a/solution.py
+++ b/solution.py
@@ -10,6 +10,7 @@
 BLOCK = 128
 TILE = 16
 WAITS = (0, 1, 3, 5)
+LATE = 0
 OUT = (0, 1, 2, 3, 4, 5, 6, 7)
 LOG2E = 1.4426950408889634
 
@@ -26,8 +27,8 @@
     return jnp.concatenate([top, bottom], axis=0)
 
 
-def local_kernel(total_length, decay, drive, a_out, e_out, f_out, q_out, ends, send,
-                 decay_v, drive_v, n_v, c_v, v_v, w_v, tile, sems):
+def local_kernel(total_length, decay, drive, gate, a_out, e_out, f_out, q_out, ends, send, gate_out,
+                 decay_v, drive_v, n_v, c_v, v_v, w_v, tile, sems, gate_sem):
     batch, length, chans = decay.shape
     blocks = length // BLOCK
     me = lax.axis_index("time")
@@ -91,6 +92,9 @@
         if s in waits:
             for which in range(2):
                 copy(which, s).wait()
+            if s == WAITS[LATE]:
+                gate_copy = pltpu.make_async_copy(gate, gate_out, gate_sem)
+                gate_copy.start()
         for b in range(batch):
             if s >= 3:
                 sums(b, s - 3)
@@ -119,6 +123,7 @@
     rightward, leftward = tile[0], tile[1]
     for k in range(send.shape[0]):
         send[k] = jnp.where(k > me, rightward, leftward)
+    gate_copy.wait()
 
 
 def states_kernel(recv, ends, a, e, f, q, gate, gated, power):
@@ -156,8 +161,8 @@
             total = None
             for k in range(2):
                 cols = pl.ds(k * half, half)
-                h = gate[b, rows, cols].astype(jnp.float32) * 0.5
-                s = (h + h * jnp.tanh(h)) * (
+                h = gate[b, rows, cols].astype(jnp.float32)
+                s = h * lax.logistic(h) * (
                     a[b, rows, cols] * (f[b, rows, cols] + alpha[k][i])
                     + e[b, rows, cols] * (beta[k][i] - q[b, rows, cols]))
                 gated[b, rows, cols] = s
@@ -200,13 +205,14 @@
     vmem = pl.BlockSpec(memory_space=pltpu.VMEM)
     hbm = pl.BlockSpec(memory_space=pltpu.HBM)
     full = jax.ShapeDtypeStruct((batch, length, chans), f32)
-    a, e, f, q, ends, send = pl.pallas_call(
+    a, e, f, q, ends, send, gate = pl.pallas_call(
         functools.partial(local_kernel, total_length),
         out_shape=(full,) * 4 + (
             jax.ShapeDtypeStruct((3, batch, blocks, chans), f32),
-            jax.ShapeDtypeStruct((devices, 8, 128), f32)),
-        in_specs=[hbm] * 2,
-        out_specs=(vmem,) * 6,
+            jax.ShapeDtypeStruct((devices, 8, 128), f32),
+            jax.ShapeDtypeStruct((batch, length, chans), jnp.bfloat16)),
+        in_specs=[hbm] * 3,
+        out_specs=(vmem,) * 7,
         scratch_shapes=[
             pltpu.VMEM((batch, length, chans), f32),
             pltpu.VMEM((batch, length, chans), jnp.bfloat16),
@@ -216,11 +222,12 @@
             pltpu.VMEM((batch, length, chans), jnp.bfloat16),
             pltpu.VMEM((2, 8, 128), f32),
             pltpu.SemaphoreType.DMA((2, blocks)),
+            pltpu.SemaphoreType.DMA,
         ],
         compiler_params=pltpu.CompilerParams(vmem_limit_bytes=32 << 20),
         name="local",
     )(*(pltpu.with_memory_space_constraint(t, pltpu.HBM)
-        for t in (decay_rate, drive_in)))
+        for t in (decay_rate, drive_in, gate_in)))
     recv = lax.all_to_all(send, "time", 0, 0)
     gated, power = pl.pallas_call(
         states_kernel,
@@ -229,7 +236,7 @@
         out_specs=(vmem,) * 2,
         compiler_params=pltpu.CompilerParams(vmem_limit_bytes=32 << 20),
         name="states",
-    )(recv, ends, a, e, f, q, gate_in)
+    )(recv, ends, a, e, f, q, gate)
     others = [
         lax.ppermute(power, "chan", [(i, i ^ k) for i in range(chan_devices)])
         for k in range(1, chan_devices)

time: 32.5 us -> 32.4 us (level)
  no operation moved by 1% of the time
where the time goes in v6:
time: 32.4 us; the launch traced here: 32.3 us
  blocking collectives  21.1 us (65%)
  Pallas kernels  5.47 us (17%)
  starting transfers between devices  3.71 us (11%)
  waiting for transfers between devices  2.01 us (6%)
    all_to_all x1, blocking collectives, on_device(): recv = lax.all_to_all(send, 'time', 0, 0)  21.1 us
    ppermute x3, starting transfers between devices, on_device(): lax.ppermute(power, 'chan', [(i, i ^ k) for i in range(chan_devices)])  3.71 us
    pallas_call x1, Pallas kernels, on_device(): pl.pallas_call(functools.partial(local_kernel, total_length), out_shape=(...  3.31 us
    ppermute x3, waiting for transfers between devices, on_device(): lax.ppermute(power, 'chan', [(i, i ^ k) for i in range(chan_devices)])  2.01 us
    pallas_call x1, Pallas kernels, on_device(): pl.pallas_call(functools.partial(scale_kernel, chans * chan_devices, floa...  1.14 us
    pallas_call x1, Pallas kernels, on_device(): pl.pallas_call(states_kernel, out_shape=(full, jax.ShapeDtypeStruct((batc...  1.02 us
  transfers between devices with their start and end apart: 3, of which 2 were waited for; matrix products, arithmetic and copies ran while one was open for 0% of the time, Pallas kernels for 0%

profile of v6, /device:TPU:1, one launch (start us, length us, event | category | flops | bytes accessed | tf_op | source)
XLA Modules:
  0.0 32.3 jit_solution(2439043485665958537)
XLA Ops:
  0.0 3.3 %local.1 = (f32[2,1024,256]{2,1,0:T(8,128)S(1)}, f32[2,1024,256]{2,1,0:T(8,128)S(1)}, f32[2,1024,256]{2,1,0:T(8,128)S(1)}, f32[2,1024,256]{2,1,0:T(8,128)S(1)}, ...) custom-call(f32[2,1024,256]{2,1,0:T(8,128)} %decay.1, ...), custom_call_target="tpu_custom_call" | custom-call | tf_op jit(solution)/shard_map/local/pallas_call | solution.py:208
  3.3 21.1 %all_to_all.5.recv = f32[32,8,128]{2,1,0:T(8,128)S(1)} all-to-all(f32[32,8,128]{2,1,0:T(8,128)S(1)} %get-tuple-element.14), channel_id=1, replica_groups=mesh['ens'=2,'time'=32,'chan'=4] {'time'}, dimensions={0} | all-to-all | bytes 262144 | tf_op jit(solution)/shard_map/all_to_all | solution.py:231
  24.4 0.0 copy-start
  24.4 1.0 %states.1 = (f32[2,1024,256]{2,1,0:T(8,128)S(1)}, f32[2,8,128]{2,1,0:T(8,128)S(1)}) custom-call(f32[32,8,128]{2,1,0:T(8,128)S(1)} %all_to_all.5.recv, f32[3,2,8,256]{3,2,1,0:T(8,128)S(1)} %get-tuple-element.15.ends, f32[2,1024,256]{2,1,0:T(8,128)S(1)} %get-tuple-element.16.a, f32[2,1024,256]{2,1,0:T(8,128)S(1)} %get-tuple-element.17.e, ...), custom_call_target="tpu_custom_call" | custom-call | tf_op jit(solution)/shard_map/states/pallas_call | solution.py:232
  25.4 3.2 %collective-permute-start.2 = (f32[2,8,128]{2,1,0:T(8,128)S(1)}, f32[2,8,128]{2,1,0:T(8,128)S(1)}, u32[]{:S(2)}, u32[]{:S(2)}) collective-permute-start(f32[2,8,128]{2,1,0:T(8,128)S(1)} %get-tuple-element.22.own), channel_id=1, source_target_pairs={{0,3},{1,2},{2,1},{3,0},{4,7},{5,6},{6,5},{7,4},{8,11},{9,10},{10,... | collective-permute-start | bytes 24584 | tf_op jit(solution)/shard_map/ppermute | solution.py:241
  28.6 0.2 collective-permute-start.1
  28.8 0.3 collective-permute-start
  29.1 1.0 %collective-permute-done.2.p3 = f32[2,8,128]{2,1,0:T(8,128)S(1)} collective-permute-done((f32[2,8,128]{2,1,0:T(8,128)S(1)}, f32[2,8,128]{2,1,0:T(8,128)S(1)}, u32[]{:S(2)}, u32[]{:S(2)}) %collective-permute-start.2) | collective-permute-done | bytes 8224 | tf_op jit(solution)/shard_map/ppermute | solution.py:241
  30.1 1.0 %collective-permute-done.1.p2 = f32[2,8,128]{2,1,0:T(8,128)S(1)} collective-permute-done((f32[2,8,128]{2,1,0:T(8,128)S(1)}, f32[2,8,128]{2,1,0:T(8,128)S(1)}, u32[]{:S(2)}, u32[]{:S(2)}) %collective-permute-start.1) | collective-permute-done | bytes 8224 | tf_op jit(solution)/shard_map/ppermute | solution.py:241
  31.1 0.0 collective-permute-done.p1
  31.1 0.0 copy-done
  31.1 1.1 %scale.1 = bf16[2,1024,256]{2,1,0:T(8,128)(2,1)} custom-call(f32[2,1024,256]{2,1,0:T(8,128)S(1)} %get-tuple-element.21.gated, f32[2,8,128]{2,1,0:T(8,128)S(1)} %get-tuple-element.22.own, f32[2,8,128]{2,1,0:T(8,128)S(1)} %collective-permute-done.p1, f32[2,8,128]{2,1,0:T(8,128)S(1)} %collective-permute-done.1.p2, f32[2,8,128]{2,1,0:T(8,128)S(1)} %collective-permute-done.2.p3, ...), custom_call_target="tpu_custom_call" | custom-call | tf_op jit(solution)/shard_map/scale/pallas_call | solution.py:244
Async XLA Ops:
  24.4 6.7 %copy-start = (f32[256]{0:T(256)S(1)}, f32[256]{0:T(256)}, u32[]{:S(2)}) copy-start(f32[256]{0:T(256)} %param.7) | copy-start | bytes 3076
  25.4 4.7 %collective-permute-start.2 = (f32[2,8,128]{2,1,0:T(8,128)S(1)}, f32[2,8,128]{2,1,0:T(8,128)S(1)}, u32[]{:S(2)}, u32[]{:S(2)}) collective-permute-start(f32[2,8,128]{2,1,0:T(8,128)S(1)} %get-tuple-element.22.own), channel_id=1, source_target_pairs={{0,3},{1,2},{2,1},{3,0},{4,7},{5,6},{6,5},{7,4},{8,11},{9,10},{10,... | collective-permute-start | bytes 24584 | tf_op jit(solution)/shard_map/ppermute | solution.py:241
  28.6 2.5 %collective-permute-start.1 = (f32[2,8,128]{2,1,0:T(8,128)S(1)}, f32[2,8,128]{2,1,0:T(8,128)S(1)}, u32[]{:S(2)}, u32[]{:S(2)}) collective-permute-start(f32[2,8,128]{2,1,0:T(8,128)S(1)} %get-tuple-element.22.own), channel_id=1, source_target_pairs={{0,2},{1,3},{2,0},{3,1},{4,6},{5,7},{6,4},{7,5},{8,10},{9,11},{10,... | collective-permute-start | bytes 24584 | tf_op jit(solution)/shard_map/ppermute | solution.py:241
  28.8 2.3 %collective-permute-start = (f32[2,8,128]{2,1,0:T(8,128)S(1)}, f32[2,8,128]{2,1,0:T(8,128)S(1)}, u32[]{:S(2)}, u32[]{:S(2)}) collective-permute-start(f32[2,8,128]{2,1,0:T(8,128)S(1)} %get-tuple-element.22.own), channel_id=1, source_target_pairs={{0,1},{1,0},{2,3},{3,2},{4,5},{5,4},{6,7},{7,6},{8,9},{9,8},{10,11... | collective-permute-start | bytes 24584 | tf_op jit(solution)/shard_map/ppermute | solution.py:241

commit v7 on v6

--- a/solution.py
+++ b/solution.py
@@ -239,7 +239,7 @@
     )(recv, ends, a, e, f, q, gate)
     others = [
         lax.ppermute(power, "chan", [(i, i ^ k) for i in range(chan_devices)])
-        for k in range(1, chan_devices)
+        for k in (1, 3, 2)
     ]
     return pl.pallas_call(
         functools.partial(scale_kernel, chans * chan_devices, float(total_length) ** -0.5),

time: 32.4 us -> 32 us (0.988)
  waiting for transfers between devices: 2.01 us -> 1.62 us
    ppermute x3, waiting for transfers between devices: 2.01 us -> 1.62 us  [on_device(): lax.ppermute(power, 'chan', [(i, i ^ k) for i in range(chan_devices)])]
  transfers between devices with their start and end apart: 3 -> 3, of which waited for: 2 -> 1; matrix products, arithmetic and copies ran while one was open for 0% -> 0% of each run, Pallas kernels for 0% -> 0%
where the time goes in v7:
time: 32 us; the launch traced here: 31.9 us
  blocking collectives  21.1 us (66%)
  Pallas kernels  5.47 us (17%)
  starting transfers between devices  3.69 us (12%)
  waiting for transfers between devices  1.62 us (5%)
    all_to_all x1, blocking collectives, on_device(): recv = lax.all_to_all(send, 'time', 0, 0)  21.1 us
    ppermute x3, starting transfers between devices, on_device(): lax.ppermute(power, 'chan', [(i, i ^ k) for i in range(chan_devices)])  3.69 us
    pallas_call x1, Pallas kernels, on_device(): pl.pallas_call(functools.partial(local_kernel, total_length), out_shape=(...  3.31 us
    ppermute x3, waiting for transfers between devices, on_device(): lax.ppermute(power, 'chan', [(i, i ^ k) for i in range(chan_devices)])  1.62 us
    pallas_call x1, Pallas kernels, on_device(): pl.pallas_call(functools.partial(scale_kernel, chans * chan_devices, floa...  1.14 us
    pallas_call x1, Pallas kernels, on_device(): pl.pallas_call(states_kernel, out_shape=(full, jax.ShapeDtypeStruct((batc...  1.02 us
  transfers between devices with their start and end apart: 3, of which 1 were waited for; matrix products, arithmetic and copies ran while one was open for 0% of the time, Pallas kernels for 0%

profile of v7, /device:TPU:1, one launch (start us, length us, event | category | flops | bytes accessed | tf_op | source)
XLA Modules:
  0.0 31.9 jit_solution(8010975490488147167)
XLA Ops:
  0.0 3.3 %local.1 = (f32[2,1024,256]{2,1,0:T(8,128)S(1)}, f32[2,1024,256]{2,1,0:T(8,128)S(1)}, f32[2,1024,256]{2,1,0:T(8,128)S(1)}, f32[2,1024,256]{2,1,0:T(8,128)S(1)}, ...) custom-call(f32[2,1024,256]{2,1,0:T(8,128)} %decay.1, ...), custom_call_target="tpu_custom_call" | custom-call | tf_op jit(solution)/shard_map/local/pallas_call | solution.py:208
  3.3 21.1 %all_to_all.5.recv = f32[32,8,128]{2,1,0:T(8,128)S(1)} all-to-all(f32[32,8,128]{2,1,0:T(8,128)S(1)} %get-tuple-element.14), channel_id=1, replica_groups=mesh['ens'=2,'time'=32,'chan'=4] {'time'}, dimensions={0} | all-to-all | bytes 262144 | tf_op jit(solution)/shard_map/all_to_all | solution.py:231
  24.4 0.0 copy-start
  24.4 1.0 %states.1 = (f32[2,1024,256]{2,1,0:T(8,128)S(1)}, f32[2,8,128]{2,1,0:T(8,128)S(1)}) custom-call(f32[32,8,128]{2,1,0:T(8,128)S(1)} %all_to_all.5.recv, f32[3,2,8,256]{3,2,1,0:T(8,128)S(1)} %get-tuple-element.15.ends, f32[2,1024,256]{2,1,0:T(8,128)S(1)} %get-tuple-element.16.a, f32[2,1024,256]{2,1,0:T(8,128)S(1)} %get-tuple-element.17.e, ...), custom_call_target="tpu_custom_call" | custom-call | tf_op jit(solution)/shard_map/states/pallas_call | solution.py:232
  25.4 1.4 %collective-permute-start.2 = (f32[2,8,128]{2,1,0:T(8,128)S(1)}, f32[2,8,128]{2,1,0:T(8,128)S(1)}, u32[]{:S(2)}, u32[]{:S(2)}) collective-permute-start(f32[2,8,128]{2,1,0:T(8,128)S(1)} %get-tuple-element.22.own), channel_id=1, source_target_pairs={{0,2},{1,3},{2,0},{3,1},{4,6},{5,7},{6,4},{7,5},{8,10},{9,11},{10,... | collective-permute-start | bytes 24584 | tf_op jit(solution)/shard_map/ppermute | solution.py:241
  26.8 2.3 %collective-permute-start.1 = (f32[2,8,128]{2,1,0:T(8,128)S(1)}, f32[2,8,128]{2,1,0:T(8,128)S(1)}, u32[]{:S(2)}, u32[]{:S(2)}) collective-permute-start(f32[2,8,128]{2,1,0:T(8,128)S(1)} %get-tuple-element.22.own), channel_id=1, source_target_pairs={{0,3},{1,2},{2,1},{3,0},{4,7},{5,6},{6,5},{7,4},{8,11},{9,10},{10,... | collective-permute-start | bytes 24584 | tf_op jit(solution)/shard_map/ppermute | solution.py:241
  29.1 0.0 collective-permute-start
  29.1 0.0 collective-permute-done.2.p3
  29.1 1.6 %collective-permute-done.1.p2 = f32[2,8,128]{2,1,0:T(8,128)S(1)} collective-permute-done((f32[2,8,128]{2,1,0:T(8,128)S(1)}, f32[2,8,128]{2,1,0:T(8,128)S(1)}, u32[]{:S(2)}, u32[]{:S(2)}) %collective-permute-start.1) | collective-permute-done | bytes 8224 | tf_op jit(solution)/shard_map/ppermute | solution.py:241
  30.7 0.0 collective-permute-done.p1
  30.7 0.0 copy-done
  30.7 1.1 %scale.1 = bf16[2,1024,256]{2,1,0:T(8,128)(2,1)} custom-call(f32[2,1024,256]{2,1,0:T(8,128)S(1)} %get-tuple-element.21.gated, f32[2,8,128]{2,1,0:T(8,128)S(1)} %get-tuple-element.22.own, f32[2,8,128]{2,1,0:T(8,128)S(1)} %collective-permute-done.p1, f32[2,8,128]{2,1,0:T(8,128)S(1)} %collective-permute-done.1.p2, f32[2,8,128]{2,1,0:T(8,128)S(1)} %collective-permute-done.2.p3, ...), custom_call_target="tpu_custom_call" | custom-call | tf_op jit(solution)/shard_map/scale/pallas_call | solution.py:244
Async XLA Ops:
  24.4 6.3 %copy-start = (f32[256]{0:T(256)S(1)}, f32[256]{0:T(256)}, u32[]{:S(2)}) copy-start(f32[256]{0:T(256)} %param.7) | copy-start | bytes 3076
  25.4 3.7 %collective-permute-start.2 = (f32[2,8,128]{2,1,0:T(8,128)S(1)}, f32[2,8,128]{2,1,0:T(8,128)S(1)}, u32[]{:S(2)}, u32[]{:S(2)}) collective-permute-start(f32[2,8,128]{2,1,0:T(8,128)S(1)} %get-tuple-element.22.own), channel_id=1, source_target_pairs={{0,2},{1,3},{2,0},{3,1},{4,6},{5,7},{6,4},{7,5},{8,10},{9,11},{10,... | collective-permute-start | bytes 24584 | tf_op jit(solution)/shard_map/ppermute | solution.py:241
  26.8 3.9 %collective-permute-start.1 = (f32[2,8,128]{2,1,0:T(8,128)S(1)}, f32[2,8,128]{2,1,0:T(8,128)S(1)}, u32[]{:S(2)}, u32[]{:S(2)}) collective-permute-start(f32[2,8,128]{2,1,0:T(8,128)S(1)} %get-tuple-element.22.own), channel_id=1, source_target_pairs={{0,3},{1,2},{2,1},{3,0},{4,7},{5,6},{6,5},{7,4},{8,11},{9,10},{10,... | collective-permute-start | bytes 24584 | tf_op jit(solution)/shard_map/ppermute | solution.py:241
  29.1 1.6 %collective-permute-start = (f32[2,8,128]{2,1,0:T(8,128)S(1)}, f32[2,8,128]{2,1,0:T(8,128)S(1)}, u32[]{:S(2)}, u32[]{:S(2)}) collective-permute-start(f32[2,8,128]{2,1,0:T(8,128)S(1)} %get-tuple-element.22.own), channel_id=1, source_target_pairs={{0,1},{1,0},{2,3},{3,2},{4,5},{5,4},{6,7},{7,6},{8,9},{9,8},{10,11... | collective-permute-start | bytes 24584 | tf_op jit(solution)/shard_map/ppermute | solution.py:241
